TPU v7x, 32 devices: a whole 2x2x4 slice. The times are simulated.
32 devices in a mesh: ha: 8 (over z, core), wa: 2 (over y), ba: 2 (over x).
Axes of the slice: x: 2, y: 2, z: 4, core: 2. Of those that a mesh axis runs over, the one named last changes fastest.
Arguments:
- tokens: bfloat16 [2, 128, 64, 384], P('ba', 'ha', 'wa'), may hold values from -6 to 6
- cotangent: bfloat16 [2, 128, 64, 384], P('ba', 'ha', 'wa'), may hold values from -6 to 6
- w_qkv: bfloat16 [384, 1152], replicated, may hold values from -0.20412415 to 0.20412415
- w_proj: bfloat16 [384, 384], replicated, may hold values from -0.3125 to 0.3125
- table_logits: float32 [12, 225], replicated, may hold values from -6 to 6
- logit_scale: float32 [12], replicated, may hold values from 1 to 5.5
- gain: float32 [384], replicated, may hold values from 0.5 to 1.5
Outputs:
- d_tokens: bfloat16 [2, 128, 64, 384], P('ba', 'ha', 'wa')
- d_wqkv: float32 [384, 1152], P(None, 'ba')
- d_wproj: float32 [384, 384], P(None, 'ba')
- d_table: float32 [12, 225], replicated
- d_scale: float32 [12], replicated
- d_gain: float32 [384], replicated
All inputs are finite; a program needn't handle non-finite values.
Results may differ from a plain program's by a relative error of at most 0.01.
The roundings to bfloat16 on the way count: a program that leaves them out, or rounds other values in their place, can miss the bound.
Values may be sent and summed in bfloat16 or wider, within the bound.
A program may use at most 64 MiB of HBM per device.

v0:
```python
import math

import functools

import jax
import jax.numpy as jnp
import numpy as np
from jax import lax
from jax.experimental import pallas as pl
from jax.experimental.pallas import tpu as pltpu
from jax.sharding import PartitionSpec as P

WIN = 8


EPS_NORM = 1e-05
MASK_FILL = -100.0
SCALE_CAP = math.log(100.0)
BIAS_RANGE = 16.0


def from_behind(block, axis, distance):
    devices = range(lax.axis_size(axis))
    route = [((i - distance) % len(devices), i) for i in devices]
    return lax.ppermute(block, axis, route)


def to_windows(block, window):
    images, height, width, depth = block.shape
    tiles = block.reshape(images, height // window, window, width // window, window, depth)
    tiles = tiles.transpose(0, 1, 3, 2, 4, 5)
    return tiles.reshape(images, height // window * (width // window), window * window, depth)


def from_windows(tiles, images, height, width, window):
    depth = tiles.shape[-1]
    grid = tiles.reshape(images, height // window, width // window, window, window, depth)
    return grid.transpose(0, 1, 3, 2, 4, 5).reshape(images, height, width, depth)


def region_of(coords, extent, window):
    return (coords >= extent - window).astype(jnp.int32) + (coords >= extent - window // 2).astype(
        jnp.int32
    )

GROUP = 4
MESH = pl.DeviceIdType.MESH
VMEM = pl.BlockSpec(memory_space=pltpu.VMEM)
NN = (((1,), (0,)), ((), ()))
NT = (((1,), (1,)), ((), ()))
TN = (((0,), (0,)), ((), ()))


def mxu(left, right, dims):
    return lax.dot_general(left, right, dims, preferred_element_type=jnp.float32)


def split(value):
    high = value.astype(jnp.bfloat16)
    return high, (value - high.astype(jnp.float32)).astype(jnp.bfloat16)


def mxu_fine(left, right, dims):
    high, low = split(left)
    return mxu(high, right, dims) + mxu(low, right, dims)


def same_block(rows, cols, row_size, col_size):
    row = lax.broadcasted_iota(jnp.int32, (rows, cols), 0) // row_size
    col = lax.broadcasted_iota(jnp.int32, (rows, cols), 1) // col_size
    return (row == col).astype(jnp.bfloat16)


def spread(value, width, length):
    tall = jnp.concatenate([value] * GROUP, 0)
    return tall * same_block(tall.shape[0], tall.shape[1], length, width)


def gather_heads(value, width, length):
    lane = lax.broadcasted_iota(jnp.int32, (length, value.shape[1]), 1) // width
    total = jnp.where(lane == 0, value[:length], 0.0)
    for head in range(1, GROUP):
        total = jnp.where(lane == head, value[head * length : (head + 1) * length], total)
    return total


def segment_max(value, size):
    lane = lax.broadcasted_iota(jnp.int32, value.shape, 1) // size
    top = jnp.zeros_like(value)
    for head in range(value.shape[1] // size):
        here = jnp.max(jnp.where(lane == head, value, -jnp.inf), -1, keepdims=True)
        top = jnp.where(lane == head, here, top)
    return top


def local_kernel(
    grid_cols, height, width, window,
    flat_ref, grad_ref, w_qkv_ref, w_proj_ref, bias_ref, scale_ref, gain_ref,
    d_flat_ref, d_wqkv_ref, d_wproj_ref, d_bias_ref, d_cos_ref, d_gain_ref,
    qkv_ref, att_ref, d_att_ref, d_qkv_ref, probs_ref, cos_ref,
):
    tokens, depth = flat_ref.shape
    length = window * window
    count = tokens // length
    groups = bias_ref.shape[0]
    lanes = depth // groups
    head_dim = lanes // GROUP
    wide = GROUP * length
    row_base = lax.axis_index("ha") * (count // grid_cols * window)
    col_base = lax.axis_index("wa") * (grid_cols * window)

    qkv_ref[...] = mxu(flat_ref[...], w_qkv_ref[...], NN).astype(jnp.bfloat16)
    lane_ones = same_block(lanes, wide, head_dim, length)
    wide_ones = same_block(wide, wide, length, length)
    lane_lane = same_block(lanes, lanes, head_dim, head_dim)
    row_ones = jnp.ones((8, lanes), jnp.bfloat16)

    def labels(place, first_row, first_col):
        place = place % length
        row = first_row + place // window
        col = first_col + place % window
        return region_of(row, height, window) * 3 + region_of(col, width, window)

    def load(w, g, part):
        return qkv_ref[
            pl.ds(pl.multiple_of(w * length, length), length),
            part * depth + g * lanes : part * depth + (g + 1) * lanes,
        ]

    def key_row_inv(tall):
        high, low = split(jnp.square(tall.astype(jnp.float32)))
        total = mxu(row_ones, high, NT) + mxu(row_ones, low, NT)
        return lax.rsqrt(total[:1] + 1.0)

    def forward(w, carry):
        first_row = row_base + w // grid_cols * window
        first_col = col_base + w % grid_cols * window
        shape = (length, wide)
        mine = labels(lax.broadcasted_iota(jnp.int32, shape, 0), first_row, first_col)
        other = labels(lax.broadcasted_iota(jnp.int32, shape, 1), first_row, first_col)
        mask = jnp.where(mine != other, MASK_FILL, 0.0)
        for g in range(groups):
            query, key, value = load(w, g, 0), load(w, g, 1), load(w, g, 2)
            tall = spread(key, head_dim, length)
            query_inv = lax.rsqrt(
                mxu_fine(jnp.square(query.astype(jnp.float32)), lane_ones, NN) + 1.0
            )
            cosine = mxu(query, tall, NT) * query_inv * key_row_inv(tall)
            scores = scale_ref[g] * cosine + bias_ref[g] + mask
            expo = jnp.exp(scores - segment_max(scores, length))
            probs = expo / mxu_fine(expo, wide_ones, NN)
            attended = mxu(probs.astype(jnp.bfloat16), spread(value, head_dim, length), NN)
            att_ref[
                pl.ds(pl.multiple_of(w * length, length), length), g * lanes : (g + 1) * lanes
            ] = attended.astype(jnp.bfloat16)
            probs_ref[w, g] = probs
            cos_ref[w, g] = cosine
        return carry

    lax.fori_loop(0, count, forward, 0)

    proj = mxu(att_ref[...], w_proj_ref[...], NN)
    centre = proj - jnp.mean(proj, -1, keepdims=True)
    inv_std = lax.rsqrt(jnp.mean(centre * centre, -1, keepdims=True) + EPS_NORM)
    normed = centre * inv_std
    upstream = grad_ref[...].astype(jnp.float32)
    d_gain_ref[...] = jnp.sum(upstream * normed, 0, keepdims=True)
    scaled = upstream * gain_ref[...]
    d_proj = inv_std * (
        scaled
        - jnp.mean(scaled, -1, keepdims=True)
        - normed * jnp.mean(scaled * normed, -1, keepdims=True)
    )
    d_proj = d_proj.astype(jnp.bfloat16)
    d_wproj_ref[...] = mxu(att_ref[...], d_proj, TN)
    d_att_ref[...] = mxu(d_proj, w_proj_ref[...], NT).astype(jnp.bfloat16)
    d_bias_ref[...] = jnp.zeros_like(d_bias_ref)
    d_cos_ref[...] = jnp.zeros_like(d_cos_ref)

    def backward(w, carry):
        rows = pl.ds(pl.multiple_of(w * length, length), length)
        for g in range(groups):
            query, key, value = load(w, g, 0), load(w, g, 1), load(w, g, 2)
            d_att = d_att_ref[rows, g * lanes : (g + 1) * lanes]
            probs = probs_ref[w, g]
            cosine = cos_ref[w, g]
            tall = spread(key, head_dim, length)
            d_probs = mxu(d_att, spread(value, head_dim, length), NT)
            d_value = gather_heads(
                mxu(probs.astype(jnp.bfloat16), d_att, TN), head_dim, length
            )
            d_scores = probs * (d_probs - mxu_fine(d_probs * probs, wide_ones, NN))
            d_bias_ref[g] += d_scores
            d_cos_ref[g] += d_scores * cosine
            scaled_scores = d_scores * scale_ref[g]
            query32, key32 = query.astype(jnp.float32), key.astype(jnp.float32)
            query_sum = mxu_fine(jnp.square(query32), lane_ones, NN)
            query_wide = lax.rsqrt(query_sum + 1.0)
            query_inv = lax.rsqrt(mxu_fine(jnp.square(query32), lane_lane, NN) + 1.0)
            key_inv = lax.rsqrt(mxu_fine(jnp.square(key32), lane_lane, NN) + 1.0)
            d_unit_q = mxu_fine(scaled_scores * key_row_inv(tall), tall, NN)
            d_unit_k = gather_heads(
                mxu_fine(scaled_scores * query_wide, query, TN), head_dim, length
            )
            unit_q, unit_k = query32 * query_inv, key32 * key_inv
            d_query = query_inv * (d_unit_q - unit_q * mxu_fine(unit_q * d_unit_q, lane_lane, NN))
            d_key = key_inv * (d_unit_k - unit_k * mxu_fine(unit_k * d_unit_k, lane_lane, NN))
            for part, grad in enumerate((d_query, d_key, d_value)):
                d_qkv_ref[rows, part * depth + g * lanes : part * depth + (g + 1) * lanes] = (
                    grad.astype(jnp.bfloat16)
                )
        return carry

    lax.fori_loop(0, count, backward, 0)
    d_wqkv_ref[...] = mxu(flat_ref[...], d_qkv_ref[...], TN)
    d_flat_ref[...] = mxu(d_qkv_ref[...], w_qkv_ref[...], NT).astype(jnp.bfloat16)


def offset_onehot(window):
    places = np.arange(window * window)
    row_of, col_of = places // window, places % window
    offset = (row_of[:, None] - row_of[None, :] + window - 1) * (2 * window - 1) + (
        col_of[:, None] - col_of[None, :] + window - 1
    )
    return jnp.asarray(offset.reshape(-1), jnp.int32)


def three_parts(value):
    high = lax.reduce_precision(value, 8, 7)
    middle = lax.reduce_precision(value - high, 8, 7)
    return jnp.concatenate([high, middle, value - high - middle], 0).astype(jnp.bfloat16)


def local_grads(block, grad_block, row_base, col_base, height, width, window, params):
    w_qkv, w_proj, table_logits, logit_scale, gain = params
    images, rows, cols, depth = block.shape
    heads = logit_scale.shape[0]
    length = window * window
    groups = heads // GROUP
    wide = GROUP * length
    flat = to_windows(block, window).reshape(-1, depth)
    grad_flat = to_windows(grad_block, window).reshape(-1, depth)
    tokens = flat.shape[0]
    count = tokens // length
    scale = jnp.exp(jnp.minimum(logit_scale, SCALE_CAP))
    scale_rows = jnp.repeat(scale.reshape(groups, GROUP), length, 1).reshape(groups, 1, wide)
    sigma = jax.nn.sigmoid(table_logits)
    entries = table_logits.shape[1]
    hot = offset_onehot(window)[None, :] == jnp.arange(entries, dtype=jnp.int32)[:, None]
    hot = hot.astype(jnp.bfloat16)
    parts = jnp.dot(three_parts(sigma * BIAS_RANGE), hot, preferred_element_type=jnp.float32)
    rel_bias = jnp.sum(parts.reshape(3, heads, -1), 0).reshape(groups, GROUP, length, length)
    rel_bias = rel_bias.transpose(0, 2, 1, 3).reshape(groups, length, wide)
    f32, b16 = jnp.float32, jnp.bfloat16
    d_flat, d_wqkv, d_wproj, d_bias, d_cos, d_gain = pl.pallas_call(
        functools.partial(local_kernel, cols // window, height, width, window),
        out_shape=[
            jax.ShapeDtypeStruct((tokens, depth), b16),
            jax.ShapeDtypeStruct((depth, 3 * depth), f32),
            jax.ShapeDtypeStruct((depth, depth), f32),
            jax.ShapeDtypeStruct((groups, length, wide), f32),
            jax.ShapeDtypeStruct((groups, length, wide), f32),
            jax.ShapeDtypeStruct((1, depth), f32),
        ],
        in_specs=[VMEM] * 7,
        out_specs=[VMEM] * 6,
        scratch_shapes=[
            pltpu.VMEM((tokens, 3 * depth), b16),
            pltpu.VMEM((tokens, depth), b16),
            pltpu.VMEM((tokens, depth), b16),
            pltpu.VMEM((tokens, 3 * depth), b16),
            pltpu.VMEM((count, groups, length, wide), f32),
            pltpu.VMEM((count, groups, length, wide), f32),
        ],
        compiler_params=pltpu.CompilerParams(vmem_limit_bytes=48 * 2**20),
        cost_estimate=pl.CostEstimate(
            flops=4_000_000_000, bytes_accessed=8_000_000, transcendentals=400_000
        ),
        name="local_grads",
    )(flat, grad_flat, w_qkv, w_proj, rel_bias, scale_rows, gain.reshape(1, depth))
    heads_bias = d_bias.reshape(groups, length, GROUP, length).transpose(0, 2, 1, 3)
    heads_bias = heads_bias.reshape(heads, length * length)
    sums = lax.dot_general(three_parts(heads_bias), hot, NT, preferred_element_type=jnp.float32)
    d_table = jnp.sum(sums.reshape(3, heads, entries), 0) * (BIAS_RANGE * sigma * (1.0 - sigma))
    live = (logit_scale < SCALE_CAP).astype(jnp.float32)
    d_scale = jnp.sum(d_cos.reshape(groups, length, GROUP, length), (1, 3)).reshape(heads)
    d_scale = d_scale * scale * live
    d_block = from_windows(d_flat.reshape(images, count, length, depth), images, rows, cols, window)
    return (d_block, (d_wqkv, d_wproj, d_table, d_scale, d_gain.reshape(depth)))


def reduce_kernel(
    shape, wqkv_ref, wproj_ref, small_ref, qkv_out, proj_out, small_out,
    core_send, core_get, image_keep, image_send, image_get, near_send, near_get, own, whole, core_all,
    small_core, small_image, small_a, small_b, small_near,
    core_sems, image_sems, near_sems, all_sems, last_sems, tiny_sems,
):
    size_h, size_w = shape
    chips = size_h // 2
    peers = chips * size_w
    ha, wa, ba = lax.axis_index("ha"), lax.axis_index("wa"), lax.axis_index("ba")
    core = ha % 2
    me = wa * chips + ha // 2
    partner = (ha + 1 - 2 * core, wa, ba)
    image = (ha, wa, 1 - ba)

    def peer(step):
        other = lax.rem(me + step, peers)
        return other, (other % chips * 2 + core, other // chips, ba)

    barrier = pltpu.get_barrier_semaphore()
    pl.semaphore_signal(barrier, inc=1, device_id=partner, device_id_type=MESH)
    pl.semaphore_signal(barrier, inc=1, device_id=image, device_id_type=MESH)
    for step in range(1, peers):
        pl.semaphore_signal(barrier, inc=1, device_id=peer(step)[1], device_id_type=MESH)

    depth = wqkv_ref.shape[0]
    half = depth // 2
    q_half, p_half = wqkv_ref.shape[1] // 2, wproj_ref.shape[1] // 2
    f32, b16 = jnp.float32, jnp.bfloat16
    mine = pl.ds(pl.multiple_of(core * half, 16), half)
    theirs = pl.ds(pl.multiple_of((1 - core) * half, 16), half)
    core_send[:, : 2 * q_half] = wqkv_ref[theirs, :].astype(b16)
    core_send[:, 2 * q_half :] = wproj_ref[theirs, :].astype(b16)
    pl.semaphore_wait(barrier, peers + 1)

    def start(src, dst, sems, device):
        copy = pltpu.make_async_remote_copy(
            src_ref=src, dst_ref=dst, send_sem=sems.at[0], recv_sem=sems.at[1],
            device_id=device, device_id_type=MESH,
        )
        copy.start()
        return copy

    big = start(core_send, core_get, core_sems, partner)
    tiny = start(small_ref, small_core, tiny_sems.at[0], partner)
    tiny.wait()
    small_a[...] = small_ref[...] + small_core[...]
    tiny = start(small_a, small_image, tiny_sems.at[1], image)
    big.wait()

    def halves(first):
        q = wqkv_ref[mine, first * q_half : (first + 1) * q_half]
        p = wproj_ref[mine, first * p_half : (first + 1) * p_half]
        gq = core_get[:, first * q_half : (first + 1) * q_half]
        gp = core_get[:, 2 * q_half + first * p_half : 2 * q_half + (first + 1) * p_half]
        return q + gq.astype(f32), p + gp.astype(f32)

    low, high = halves(0), halves(1)
    for part, (a, b) in enumerate(zip(low, high)):
        place = slice(0, q_half) if part == 0 else slice(q_half, q_half + p_half)
        image_send[:, place] = jnp.where(ba == 0, b, a).astype(b16)
        image_keep[:, place] = jnp.where(ba == 0, a, b)
    big = start(image_send, image_get, image_sems, image)
    tiny.wait()
    small_b[...] = small_a[...] + small_image[...]
    tinies = []
    for step in range(1, peers):
        tinies.append(start(small_b, small_near.at[step - 1], tiny_sems.at[step + 1], peer(step)[1]))
    big.wait()
    total = image_keep[...] + image_get[...].astype(f32)
    r, c = near_send.shape[1:]
    split_c = total.shape[1] // c
    for j in range(peers):
        row, col = j // split_c * r, j % split_c * c
        near_send[j] = total[row : row + r, col : col + c].astype(b16)
    copies = []
    for step in range(1, peers):
        other, device = peer(step)
        copies.append(start(near_send.at[other], near_get.at[step - 1], near_sems.at[step - 1], device))
    for copy in tinies:
        copy.wait()
    small = small_b[...]
    for step in range(1, peers):
        small = small + small_near[step - 1]
    small_out[...] = small
    for copy in copies:
        copy.wait()
    total = near_send[me].astype(f32)
    for step in range(1, peers):
        total = total + near_get[step - 1].astype(f32)
    own[...] = total.astype(b16)
    whole[me] = own[...]
    copies = []
    for step in range(1, peers):
        _, device = peer(step)
        copies.append(start(own, whole.at[me], all_sems.at[step - 1], device))
    for copy in copies:
        copy.wait()
    last = start(whole, core_all, last_sems, partner)

    def put(source, first):
        for j in range(peers):
            row, col = j // split_c * r, j % split_c * c
            block = source[j].astype(f32)
            rows = pl.ds(pl.multiple_of(first * half + row, 8), r)
            q_part = max(0, min(c, q_half - col))
            if q_part > 0:
                qkv_out[rows, col : col + q_part] = block[:, :q_part]
            if q_part < c:
                begin = col + q_part - q_half
                proj_out[rows, begin : begin + c - q_part] = block[:, q_part:]

    put(whole, core)
    last.wait()
    put(core_all, 1 - core)


def reduce_all(d_wqkv, d_wproj, small):
    size_h, size_w = lax.axis_size("ha"), lax.axis_size("wa")
    peers = size_h // 2 * size_w
    depth = d_wqkv.shape[0]
    half = depth // 2
    cols = (d_wqkv.shape[1] + d_wproj.shape[1]) // 2
    split_c = 2
    r, c = half * split_c // peers, cols // split_c
    f32, b16 = jnp.float32, jnp.bfloat16
    tiny = small.shape
    return pl.pallas_call(
        functools.partial(reduce_kernel, (size_h, size_w)),
        out_shape=[
            jax.ShapeDtypeStruct((depth, d_wqkv.shape[1] // 2), f32),
            jax.ShapeDtypeStruct((depth, d_wproj.shape[1] // 2), f32),
            jax.ShapeDtypeStruct(tiny, f32),
        ],
        in_specs=[VMEM] * 3,
        out_specs=[VMEM] * 3,
        scratch_shapes=[
            pltpu.VMEM((half, 2 * cols), b16),
            pltpu.VMEM((half, 2 * cols), b16),
            pltpu.VMEM((half, cols), f32),
            pltpu.VMEM((half, cols), b16),
            pltpu.VMEM((half, cols), b16),
            pltpu.VMEM((peers, r, c), b16),
            pltpu.VMEM((peers - 1, r, c), b16),
            pltpu.VMEM((r, c), b16),
            pltpu.VMEM((peers, r, c), b16),
            pltpu.VMEM((peers, r, c), b16),
            pltpu.VMEM(tiny, f32),
            pltpu.VMEM(tiny, f32),
            pltpu.VMEM(tiny, f32),
            pltpu.VMEM(tiny, f32),
            pltpu.VMEM((peers - 1, *tiny), f32),
            pltpu.SemaphoreType.DMA((2,)),
            pltpu.SemaphoreType.DMA((2,)),
            pltpu.SemaphoreType.DMA((peers - 1, 2)),
            pltpu.SemaphoreType.DMA((peers - 1, 2)),
            pltpu.SemaphoreType.DMA((2,)),
            pltpu.SemaphoreType.DMA((peers + 1, 2)),
        ],
        compiler_params=pltpu.CompilerParams(
            collective_id=0, has_side_effects=True, vmem_limit_bytes=48 * 2**20
        ),
        name="reduce_all",
    )(d_wqkv, d_wproj, small)


def can_reduce(d_wqkv):
    peers = lax.axis_size("ha") // 2 * lax.axis_size("wa")
    pairs = lax.axis_size("ha") % 2 == 0 and lax.axis_size("ba") == 2
    return pairs and peers > 1 and d_wqkv.shape[0] % peers == 0 and d_wqkv.shape[0] // peers % 16 == 0


def pack_small(d_table, d_scale, d_gain):
    heads, entries = d_table.shape
    lanes = -(-entries // 128) * 128
    flat = jnp.concatenate([d_scale, d_gain])
    rows = -(-flat.shape[0] // lanes)
    flat = jnp.pad(flat, (0, rows * lanes - flat.shape[0])).reshape(rows, lanes)
    table = jnp.pad(d_table, ((0, 0), (0, lanes - entries)))
    full = jnp.concatenate([table, flat], 0)
    return jnp.pad(full, ((0, -full.shape[0] % 8), (0, 0)))


def unpack_small(full, heads, entries, depth):
    flat = full[heads:].reshape(-1)
    return full[:heads, :entries], flat[:heads], flat[heads : heads + depth]


def shift_in(tokens, cotangent, shift):
    stacked = jnp.stack([tokens, cotangent])
    below = from_behind(stacked[:, :, :shift], "ha", -1)
    tall = jnp.concatenate([stacked[:, :, shift:], below], 2)
    beside = from_behind(tall[:, :, :, :shift], "wa", -1)
    moved = jnp.concatenate([tall[:, :, :, shift:], beside], 3)
    return (moved[0], moved[1])


def shift_out(grads, shift):
    rows = grads.shape[1]
    cols = grads.shape[2]
    right = from_behind(grads[:, :, cols - shift :], "wa", 1)
    wide = jnp.concatenate([right, grads[:, :, : cols - shift]], 2)
    lower = from_behind(wide[:, rows - shift :], "ha", 1)
    return jnp.concatenate([lower, wide[:, : rows - shift]], 1)


def shards(tokens, cotangent, w_qkv, w_proj, table_logits, logit_scale, gain):
    rows = tokens.shape[1]
    cols = tokens.shape[2]
    shift = WIN // 2
    height = rows * lax.axis_size("ha")
    width = cols * lax.axis_size("wa")
    row_base = lax.axis_index("ha") * rows
    col_base = lax.axis_index("wa") * cols
    params = (w_qkv, w_proj, table_logits, logit_scale, gain)
    moved, moved_grad = shift_in(tokens, cotangent, shift)
    d_moved, parts = local_grads(moved, moved_grad, row_base, col_base, height, width, WIN, params)
    back = shift_out(d_moved, shift)
    d_tokens = (cotangent.astype(jnp.float32) + back.astype(jnp.float32)).astype(jnp.bfloat16)
    d_wqkv, d_wproj, d_table, d_scale, d_gain = parts
    if can_reduce(d_wqkv):
        small = pack_small(d_table, d_scale, d_gain)
        half_qkv, half_proj, small = reduce_all(d_wqkv, d_wproj, small)
        d_table, d_scale, d_gain = unpack_small(small, *d_table.shape, d_gain.shape[0])
    else:
        half_qkv, half_proj = (
            lax.psum_scatter(d_wqkv.astype(jnp.bfloat16), "ba", scatter_dimension=1, tiled=True).astype(
                jnp.float32
            ),
            lax.psum_scatter(
                d_wproj.astype(jnp.bfloat16), "ba", scatter_dimension=1, tiled=True
            ).astype(jnp.float32),
        )
        half_qkv, half_proj = lax.psum((half_qkv, half_proj), ("ha", "wa"))
        d_table, d_scale, d_gain = lax.psum((d_table, d_scale, d_gain), ("ha", "wa", "ba"))
    return (d_tokens, half_qkv, half_proj, d_table, d_scale, d_gain)


def solution(mesh):
    return jax.shard_map(
        shards,
        mesh=mesh,
        in_specs=(P("ba", "ha", "wa", None), P("ba", "ha", "wa", None), P(), P(), P(), P(), P()),
        out_specs=(P("ba", "ha", "wa", None), P(None, "ba"), P(None, "ba"), P(), P(), P()),
        check_vma=False,
    )
```

profile of v0, /device:TPU:0, one launch (start us, length us, event | category | flops | bytes accessed | tf_op | source)
XLA Modules:
  0.0 87.6 jit_solution(4728340465275639193)
XLA Ops:
  0.7 1.0 %pad_maximum_fusion.2 = bf16[2,1,4,32,384]{4,3,2,1,0:T(8,128)(2,1)S(1)} fusion(bf16[1,1,16,32,384]{4,3,2,1,0:T(8,128)(2,1)} %bitcast.32, bf16[1,1,16,32,384]{4,3,2,1,0:T(8,128)(2,1)} %bitcast.38), kind=kLoop, calls=%fused_computation.27 | loop fusion | flops 98304 | bytes 983040 | tf_op jit(solution)/shard_map/stack | solution.py:481
  1.6 4.6 %collective-permute-start = (bf16[2,1,4,32,384]{4,3,2,1,0:T(8,128)(2,1)S(1)}, bf16[2,1,4,32,384]{4,3,2,1,0:T(8,128)(2,1)S(1)}, u32[]{:S(2)}, u32[]{:S(2)}) collective-permute-start(bf16[2,1,4,32,384]{4,3,2,1,0:T(8,128)(2,1)S(1)} %pad_maximum_fusion.2), channel_id=1, source_target_pairs={{4,0},{8,4},{12,8},{16,12},{20,16},{24,20},{28,24},{0,28},{5,1},{9... | collective-permute-start | bytes 589832 | tf_op jit(solution)/shard_map/ppermute | solution.py:25
  6.2 0.7 reduce-precision_convert_fusion.3
  6.9 1.5 %fusion.1 = f32[36,4096]{1,0:T(8,128)S(1)} fusion(s32[4096]{0:T(1024)} %constant.13.clone, bf16[12,225]{1,0:T(8,128)(2,1)S(1)} %get-tuple-element.48, bf16[12,225]{1,0:T(8,128)(2,1)S(1)} %get-tuple-element.49, bf16[12,225]{1,0:T(8,128)(2,1)S(1)} %get-tuple-element.47), kind=kOutput, calls=%fused_computation.2 | convolution fusion | flops 67325400 | bytes 622408 | tf_op jit(solution)/shard_map/dot_general | solution.py:251
  8.6 0.1 reshape_reshape.14.scale_ref
  8.8 0.2 reshape.83
  9.0 0.3 copy.28
  9.3 0.3 reshape.84.bias_ref
  9.5 0.2 copy-done.7
  9.7 0.1 copy-done.9
  10.0 1.6 %collective-permute-start.1 = (bf16[2,1,16,4,384]{4,3,2,1,0:T(4,128)(2,1)S(1)}, bf16[2,1,16,4,384]{4,3,2,1,0:T(4,128)(2,1)S(1)}, u32[]{:S(2)}, u32[]{:S(2)}) collective-permute-start(bf16[2,1,16,4,384]{4,3,2,1,0:T(4,128)(2,1)S(1)} %pad_maximum_fusion.4), channel_id=1, source_target_pairs={{2,0},{0,2},{3,1},{1,3},{6,4},{4,6},{7,5},{5,7},{10,8},{8,10},{11,... | collective-permute-start | bytes 294920 | tf_op jit(solution)/shard_map/ppermute | solution.py:25
  11.6 0.2 slice_maximum_fusion
  11.8 2.8 %collective-permute-done.1 = bf16[2,1,16,4,384]{4,3,2,1,0:T(4,128)(2,1)S(1)} collective-permute-done((bf16[2,1,16,4,384]{4,3,2,1,0:T(4,128)(2,1)S(1)}, bf16[2,1,16,4,384]{4,3,2,1,0:T(4,128)(2,1)S(1)}, u32[]{:S(2)}, u32[]{:S(2)}) %collective-permute-start.1) | collective-permute-done | bytes 98336 | tf_op jit(solution)/shard_map/ppermute | solution.py:25
  14.7 0.1 pad_maximum_fusion.1
  14.9 29.8 %local_grads.1 = (bf16[512,384]{1,0:T(8,128)(2,1)S(1)}, f32[384,1152]{1,0:T(8,128)S(1)}, f32[384,384]{1,0:T(8,128)S(1)}, f32[3,64,256]{2,1,0:T(8,128)S(1)}, f32[...) custom-call(bf16[512,384]{1,0:T(8,128)(2,1)S(1)} %bitcast.26, bf16[512,384]{1,0:T(8,128)(2,1)S(1)} %bitcast.25, ...), custom_call_target="tpu_custom_call" | custom-call | flops 4000000000 | bytes 8000000 | tf_op jit(solution)/shard_map/local_grads/pallas_call | solution.py:255
  44.9 0.1 reduce_sum.38
  45.0 0.1 reshape.91
  45.3 1.6 %collective-permute-start.2 = (bf16[1,16,4,384]{3,2,1,0:T(4,128)(2,1)S(1)}, bf16[1,16,4,384]{3,2,1,0:T(4,128)(2,1)S(1)}, u32[]{:S(2)}, u32[]{:S(2)}) collective-permute-start(bf16[1,16,4,384]{3,2,1,0:T(4,128)(2,1)S(1)} %slice.62), channel_id=1, source_target_pairs={{2,0},{0,2},{3,1},{1,3},{6,4},{4,6},{7,5},{5,7},{10,8},{8,10},{11,... | collective-permute-start | bytes 147464 | tf_op jit(solution)/shard_map/ppermute | solution.py:25
  46.8 0.2 reshape.88
  47.0 0.8 copy.35
  47.8 1.1 %reshape.89 = f32[12,4096]{1,0:T(8,128)S(1)} reshape(f32[3,4,64,64]{3,2,1,0:T(8,128)} %bitcast.35) | data formatting | bytes 393216 | tf_op jit(solution)/shard_map/reshape | solution.py:282
  49.1 0.8 fusion
  50.0 29.4 %reduce_all.1 = (f32[384,576]{1,0:T(8,128)S(1)}, f32[384,192]{1,0:T(8,128)S(1)}, f32[16,256]{1,0:T(8,128)S(1)}) custom-call(f32[384,1152]{1,0:T(8,128)S(1)} %get-tuple-element.16.wqkv_ref, f32[384,384]{1,0:T(8,128)S(1)} %get-tuple-element.17.wproj_ref, f32[16,256]{1,0:T(8,128)S(1)} %pad.14.small_ref), custom_call_target="tpu_custom_call" | custom-call | tf_op jit(solution)/shard_map/reduce_all/pallas_call | solution.py:419
  79.3 0.7 copy-done
  80.1 0.4 collective-permute-start.3
  80.6 0.5 slice.54
  81.1 0.6 slice.55
  81.7 1.2 %copy.31 = f32[384,576]{0,1:T(8,128)} copy(f32[384,576]{1,0:T(8,128)S(1)} %get-tuple-element.37) | data formatting | bytes 1769472
  83.0 0.9 copy.32
  83.8 2.2 %collective-permute-done.3 = bf16[1,4,32,384]{3,2,1,0:T(8,128)(2,1)S(1)} collective-permute-done((bf16[1,4,32,384]{3,2,1,0:T(8,128)(2,1)S(1)}, bf16[1,4,32,384]{3,2,1,0:T(8,128)(2,1)S(1)}, u32[]{:S(2)}, u32[]{:S(2)}) %collective-permute-start.3) | collective-permute-done | bytes 98336 | tf_op jit(solution)/shard_map/ppermute | solution.py:25
  86.0 0.9 %add_convert_fusion = bf16[1,16,32,384]{3,2,1,0:T(8,128)(2,1)} fusion(bf16[1,16,32,384]{3,2,1,0:T(8,128)(2,1)S(1)} %copy-done.8, bf16[1,16,28,384]{3,2,1,0:T(8,128)(2,1)S(1)} %bitcast.31, bf16[1,16,4,384]{3,2,1,0:T(4,128)(2,1)S(1)} %collective-permute-done.2, bf16[1,4,32,384]{3,2,1,0:T(8,128)(2,1)S(1)} %collective-permute-done.3), kind=kLoop, calls=%fused_computation.10 | loop fusion | flops 1769472 | bytes 1277952 | tf_op jit(solution)/shard_map/convert_element_type | solution.py:510
  87.0 0.6 copy.37
  (54 shorter events, 1.0 us)
Async XLA Ops:
  0.6 7.8 %copy-start.12 = (f32[12]{0:T(128)S(1)}, f32[12]{0:T(128)}, u32[]{:S(2)}) copy-start(f32[12]{0:T(128)} %param.13) | copy-start | bytes 148
  0.6 7.9 %copy-start.11 = (f32[384]{0:T(512)S(1)}, f32[384]{0:T(512)}, u32[]{:S(2)}) copy-start(f32[384]{0:T(512)} %param.14) | copy-start | bytes 4612
  1.6 8.3 %collective-permute-start = (bf16[2,1,4,32,384]{4,3,2,1,0:T(8,128)(2,1)S(1)}, bf16[2,1,4,32,384]{4,3,2,1,0:T(8,128)(2,1)S(1)}, u32[]{:S(2)}, u32[]{:S(2)}) collective-permute-start(bf16[2,1,4,32,384]{4,3,2,1,0:T(8,128)(2,1)S(1)} %pad_maximum_fusion.2), channel_id=1, source_target_pairs={{4,0},{8,4},{12,8},{16,12},{20,16},{24,20},{28,24},{0,28},{5,1},{9... | collective-permute-start | bytes 589832 | tf_op jit(solution)/shard_map/ppermute | solution.py:25
  8.7 1.0 %copy-start.7 = (bf16[1,16,32,384]{3,2,1,0:T(8,128)(2,1)S(1)}, bf16[1,16,32,384]{3,2,1,0:T(8,128)(2,1)}, u32[]{:S(2)}) copy-start(bf16[1,16,32,384]{3,2,1,0:T(8,128)(2,1)} %param.9) | copy-start | bytes 1179652
  8.8 1.1 %copy-start.9 = (bf16[1,16,32,384]{3,2,1,0:T(8,128)(2,1)S(1)}, bf16[1,16,32,384]{3,2,1,0:T(8,128)(2,1)}, u32[]{:S(2)}) copy-start(bf16[1,16,32,384]{3,2,1,0:T(8,128)(2,1)} %param.8) | copy-start | bytes 1179652
  10.0 4.7 %collective-permute-start.1 = (bf16[2,1,16,4,384]{4,3,2,1,0:T(4,128)(2,1)S(1)}, bf16[2,1,16,4,384]{4,3,2,1,0:T(4,128)(2,1)S(1)}, u32[]{:S(2)}, u32[]{:S(2)}) collective-permute-start(bf16[2,1,16,4,384]{4,3,2,1,0:T(4,128)(2,1)S(1)} %pad_maximum_fusion.4), channel_id=1, source_target_pairs={{2,0},{0,2},{3,1},{1,3},{6,4},{4,6},{7,5},{5,7},{10,8},{8,10},{11,... | collective-permute-start | bytes 294920 | tf_op jit(solution)/shard_map/ppermute | solution.py:25
  11.8 3.1 %copy-start.2 = (bf16[384,1152]{1,0:T(8,128)(2,1)S(1)}, bf16[384,1152]{1,0:T(8,128)(2,1)}, u32[]{:S(2)}) copy-start(bf16[384,1152]{1,0:T(8,128)(2,1)} %w_qkv_ref.1) | copy-start | bytes 2654212
  11.8 3.1 %copy-start.3 = (bf16[384,384]{1,0:T(8,128)(2,1)S(1)}, bf16[384,384]{1,0:T(8,128)(2,1)}, u32[]{:S(2)}) copy-start(bf16[384,384]{1,0:T(8,128)(2,1)} %w_proj_ref.1) | copy-start | bytes 884740
  44.7 4.3 %copy-start.13 = (s32[4096]{0:T(1024)S(1)}, s32[4096]{0:T(1024)}, u32[]{:S(2)}) copy-start(s32[4096]{0:T(1024)} %constant.13.clone) | copy-start | bytes 49156
  44.8 5.1 %copy-start.4 = (bf16[1,2,8,4,8,384]{5,4,3,2,1,0:T(8,128)(2,1)}, bf16[1,2,8,4,8,384]{5,4,3,2,1,0:T(8,128)(2,1)S(1)}, u32[]{:S(2)}) copy-start(bf16[1,2,8,4,8,384]{5,4,3,2,1,0:T(8,128)(2,1)S(1)} %copy.29) | copy-start | bytes 1179652
  45.3 34.8 %collective-permute-start.2 = (bf16[1,16,4,384]{3,2,1,0:T(4,128)(2,1)S(1)}, bf16[1,16,4,384]{3,2,1,0:T(4,128)(2,1)S(1)}, u32[]{:S(2)}, u32[]{:S(2)}) collective-permute-start(bf16[1,16,4,384]{3,2,1,0:T(4,128)(2,1)S(1)} %slice.62), channel_id=1, source_target_pairs={{2,0},{0,2},{3,1},{1,3},{6,4},{4,6},{7,5},{5,7},{10,8},{8,10},{11,... | collective-permute-start | bytes 147464 | tf_op jit(solution)/shard_map/ppermute | solution.py:25
  47.8 2.1 %copy-start.10 = (f32[12,225]{1,0:T(8,128)S(1)}, f32[12,225]{1,0:T(8,128)}, u32[]{:S(2)}) copy-start(f32[12,225]{1,0:T(8,128)} %param.12) | copy-start | bytes 32404
  49.9 30.2 %copy-start.5 = (bf16[1,2,8,4,8,384]{5,4,3,2,1,0:T(8,128)(2,1)S(1)}, bf16[1,2,8,4,8,384]{5,4,3,2,1,0:T(8,128)(2,1)}, u32[]{:S(2)}) copy-start(bf16[1,2,8,4,8,384]{5,4,3,2,1,0:T(8,128)(2,1)} %copy-done.4) | copy-start | bytes 1179652
  79.3 0.7 copy-start
  80.1 6.0 %copy-start.6 = (bf16[1,2,8,4,8,384]{5,4,3,2,1,0:T(8,128)(2,1)S(1)}, bf16[1,2,8,4,8,384]{5,4,3,2,1,0:T(8,128)(2,1)}, u32[]{:S(2)}) copy-start(bf16[1,2,8,4,8,384]{5,4,3,2,1,0:T(8,128)(2,1)} %copy-done.4) | copy-start | bytes 1179652
  80.1 6.0 %copy-start.8 = (bf16[1,16,32,384]{3,2,1,0:T(8,128)(2,1)S(1)}, bf16[1,16,32,384]{3,2,1,0:T(8,128)(2,1)}, u32[]{:S(2)}) copy-start(bf16[1,16,32,384]{3,2,1,0:T(8,128)(2,1)} %param.9) | copy-start | bytes 1179652
  80.1 2.9 %copy-start.1 = (f32[384,192]{1,0:T(8,128)S(1)}, f32[384,192]{1,0:T(8,128)}, u32[]{:S(2)}) copy-start(f32[384,192]{1,0:T(8,128)} %copy-done) | copy-start | bytes 884740
  80.1 5.9 %collective-permute-start.3 = (bf16[1,4,32,384]{3,2,1,0:T(8,128)(2,1)S(1)}, bf16[1,4,32,384]{3,2,1,0:T(8,128)(2,1)S(1)}, u32[]{:S(2)}, u32[]{:S(2)}) collective-permute-start(bf16[1,4,32,384]{3,2,1,0:T(8,128)(2,1)S(1)} %pad_maximum_fusion.3), channel_id=1, source_target_pairs={{28,0},{0,4},{4,8},{8,12},{12,16},{16,20},{20,24},{24,28},{29,1},{... | collective-permute-start | bytes 294920 | tf_op jit(solution)/shard_map/ppermute | solution.py:25
where the time goes:
time: 87.9 us; the launch traced here: 87.6 us
  Pallas kernels  59.1 us (67%)
  local copies, waits for them, and re-layouts  8.47 us (10%)
  starting transfers between devices  8.16 us (9%)
  waiting for transfers between devices  5.02 us (6%)
  other arithmetic  3.52 us (4%)
  matrix products  2.26 us (3%)
  between operations  0.98 us (1%)
    pallas_call x1, Pallas kernels, local_grads(): pl.pallas_call(functools.partial(local_kernel, cols // window, height, wi...  29.8 us
    pallas_call x1, Pallas kernels, reduce_all(): pl.pallas_call(functools.partial(reduce_kernel, (size_h, size_w)), out_sh...  29.4 us
    ppermute x4, starting transfers between devices, from_behind(): return lax.ppermute(block, axis, route)  8.16 us
    ppermute x4, waiting for transfers between devices, from_behind(): return lax.ppermute(block, axis, route)  5.02 us
    unnamed x33, local copies, waits for them, and re-layouts  3.85 us
  transfers between devices with their start and end apart: 4, of which 2 were waited for; matrix products, arithmetic and copies ran while one was open for 11% of the time, Pallas kernels for 34%

commit v1 on v0

--- a/solution.py
+++ b/solution.py
@@ -44,6 +44,9 @@
     )
 
 GROUP = 4
+FWD = 2
+BWD = 4
+LOG2E = math.log2(math.e)
 MESH = pl.DeviceIdType.MESH
 VMEM = pl.BlockSpec(memory_space=pltpu.VMEM)
 NN = (((1,), (0,)), ((), ()))
@@ -71,99 +74,114 @@
     return (row == col).astype(jnp.bfloat16)
 
 
-def spread(value, width, length):
-    tall = jnp.concatenate([value] * GROUP, 0)
-    return tall * same_block(tall.shape[0], tall.shape[1], length, width)
+def tile_heads(value, width, reps):
+    lane = lax.broadcasted_iota(jnp.int32, (1, value.shape[1]), 1) % (GROUP * width) // width
+    rows = []
+    for head in range(GROUP):
+        rows.append(value * (lane == head).astype(jnp.bfloat16))
+    return jnp.concatenate(rows, 0)
 
 
 def gather_heads(value, width, length):
     lane = lax.broadcasted_iota(jnp.int32, (length, value.shape[1]), 1) // width
-    total = jnp.where(lane == 0, value[:length], 0.0)
+    total = value[:length]
     for head in range(1, GROUP):
         total = jnp.where(lane == head, value[head * length : (head + 1) * length], total)
     return total
-
-
-def segment_max(value, size):
-    lane = lax.broadcasted_iota(jnp.int32, value.shape, 1) // size
-    top = jnp.zeros_like(value)
-    for head in range(value.shape[1] // size):
-        here = jnp.max(jnp.where(lane == head, value, -jnp.inf), -1, keepdims=True)
-        top = jnp.where(lane == head, here, top)
-    return top
 
 
 def local_kernel(
     grid_cols, height, width, window,
     flat_ref, grad_ref, w_qkv_ref, w_proj_ref, bias_ref, scale_ref, gain_ref,
     d_flat_ref, d_wqkv_ref, d_wproj_ref, d_bias_ref, d_cos_ref, d_gain_ref,
-    qkv_ref, att_ref, d_att_ref, d_qkv_ref, probs_ref, cos_ref,
+    qkv_ref, att_ref, d_att_ref, d_qkv_ref, probs_ref, kinv_ref, qrow_ref, masked_ref, raw_q_ref, raw_k_ref,
+    norm_ref,
 ):
     tokens, depth = flat_ref.shape
+    f32, b16 = jnp.float32, jnp.bfloat16
     length = window * window
     count = tokens // length
     groups = bias_ref.shape[0]
     lanes = depth // groups
+    heads = groups * GROUP
     head_dim = lanes // GROUP
     wide = GROUP * length
     row_base = lax.axis_index("ha") * (count // grid_cols * window)
     col_base = lax.axis_index("wa") * (grid_cols * window)
 
-    qkv_ref[...] = mxu(flat_ref[...], w_qkv_ref[...], NN).astype(jnp.bfloat16)
+    qkv_ref[...] = mxu(flat_ref[...], w_qkv_ref[...], NN).astype(b16)
     lane_ones = same_block(lanes, wide, head_dim, length)
-    wide_ones = same_block(wide, wide, length, length)
     lane_lane = same_block(lanes, lanes, head_dim, head_dim)
-    row_ones = jnp.ones((8, lanes), jnp.bfloat16)
-
-    def labels(place, first_row, first_col):
-        place = place % length
-        row = first_row + place // window
-        col = first_col + place % window
-        return region_of(row, height, window) * 3 + region_of(col, width, window)
-
-    def load(w, g, part):
-        return qkv_ref[
+
+    head_rows = scale_ref.shape[0]
+    pick = same_block(head_rows, depth, 1, head_dim)
+    high, low = split(jnp.square(qkv_ref[:, :depth].astype(f32)))
+    q_sums = mxu(pick, high, NT) + mxu(pick, low, NT)
+    q_rows = lax.rsqrt(q_sums + 1.0) * scale_ref[:, :1]
+    half = lax.broadcasted_iota(jnp.int32, (1, 2 * length), 1) < length
+    for j in range(count // 2):
+        base = q_rows[:, j * 2 * length : (j + 1) * 2 * length]
+        turned = pltpu.roll(base, length, 1)
+        for g in range(groups):
+            for p in range(GROUP // 2):
+                one, two = g * GROUP + 2 * p, g * GROUP + 2 * p + 1
+                place = slice(p * 2 * length, (p + 1) * 2 * length)
+                qrow_ref[2 * j, g, :, place] = jnp.where(half, base[one : one + 1], turned[two : two + 1])
+                qrow_ref[2 * j + 1, g, :, place] = jnp.where(half, turned[one : one + 1], base[two : two + 1])
+    for g in range(groups):
+        query = qkv_ref[:, g * lanes : (g + 1) * lanes].astype(f32)
+        key = qkv_ref[:, depth + g * lanes : depth + (g + 1) * lanes].astype(f32)
+        high, low = split(jnp.square(key))
+        kinv_ref[g] = lax.rsqrt(mxu(high, lane_ones, NN) + mxu(low, lane_ones, NN) + 1.0)
+        norm_ref[1, g] = 1.0 / (mxu(high, lane_lane, NN) + mxu(low, lane_lane, NN) + 1.0)
+        high, low = split(jnp.square(query))
+        norm_ref[0, g] = 1.0 / (mxu(high, lane_lane, NN) + mxu(low, lane_lane, NN) + 1.0)
+
+    mine = lax.broadcasted_iota(jnp.int32, (length, wide), 0)
+    other = lax.broadcasted_iota(jnp.int32, (length, wide), 1) % length
+    cut = window // 2
+    row_off = (mine // window // cut) != (other // window // cut)
+    col_off = (mine % window // cut) != (other % window // cut)
+    for g in range(groups):
+        bias = bias_ref[g] * LOG2E
+        masked_ref[0, g] = bias
+        masked_ref[1, g] = jnp.where(col_off, bias + MASK_FILL * LOG2E, bias)
+        masked_ref[2, g] = jnp.where(row_off, bias + MASK_FILL * LOG2E, bias)
+        masked_ref[3, g] = jnp.where(row_off | col_off, bias + MASK_FILL * LOG2E, bias)
+
+    def load(ref, w, g, part):
+        return ref[
             pl.ds(pl.multiple_of(w * length, length), length),
             part * depth + g * lanes : part * depth + (g + 1) * lanes,
         ]
 
-    def key_row_inv(tall):
-        high, low = split(jnp.square(tall.astype(jnp.float32)))
-        total = mxu(row_ones, high, NT) + mxu(row_ones, low, NT)
-        return lax.rsqrt(total[:1] + 1.0)
-
-    def forward(w, carry):
-        first_row = row_base + w // grid_cols * window
-        first_col = col_base + w % grid_cols * window
-        shape = (length, wide)
-        mine = labels(lax.broadcasted_iota(jnp.int32, shape, 0), first_row, first_col)
-        other = labels(lax.broadcasted_iota(jnp.int32, shape, 1), first_row, first_col)
-        mask = jnp.where(mine != other, MASK_FILL, 0.0)
-        for g in range(groups):
-            query, key, value = load(w, g, 0), load(w, g, 1), load(w, g, 2)
-            tall = spread(key, head_dim, length)
-            query_inv = lax.rsqrt(
-                mxu_fine(jnp.square(query.astype(jnp.float32)), lane_ones, NN) + 1.0
-            )
-            cosine = mxu(query, tall, NT) * query_inv * key_row_inv(tall)
-            scores = scale_ref[g] * cosine + bias_ref[g] + mask
-            expo = jnp.exp(scores - segment_max(scores, length))
-            probs = expo / mxu_fine(expo, wide_ones, NN)
-            attended = mxu(probs.astype(jnp.bfloat16), spread(value, head_dim, length), NN)
+    def forward(step, carry):
+        units = [(step * FWD + k, g) for k in range(FWD) for g in range(groups)]
+        scores = []
+        for w, g in units:
+            query, key = load(qkv_ref, w, g, 0), load(qkv_ref, w, g, 1)
+            raw = mxu(key, tile_heads(query, head_dim, length), NT)
+            last_row = (row_base + w // grid_cols * window) // (height - window)
+            last_col = (col_base + w % grid_cols * window) // (width - window)
+            kinv = kinv_ref[g, pl.ds(pl.multiple_of(w * length, length), length), :]
+            scores.append(raw * kinv * (qrow_ref[w, g] * LOG2E) + masked_ref[last_row * 2 + last_col, g])
+        for (w, g), score in zip(units, scores):
+            expo = jnp.exp2(score - jnp.max(score, 0, keepdims=True))
+            probs = expo * (1.0 / jnp.sum(expo, 0, keepdims=True))
+            probs_ref[w, g] = probs
+            att = gather_heads(mxu(probs.astype(b16), load(qkv_ref, w, g, 2), TN), head_dim, length)
             att_ref[
                 pl.ds(pl.multiple_of(w * length, length), length), g * lanes : (g + 1) * lanes
-            ] = attended.astype(jnp.bfloat16)
-            probs_ref[w, g] = probs
-            cos_ref[w, g] = cosine
+            ] = att.astype(b16)
         return carry
 
-    lax.fori_loop(0, count, forward, 0)
+    lax.fori_loop(0, count // FWD, forward, 0)
 
     proj = mxu(att_ref[...], w_proj_ref[...], NN)
     centre = proj - jnp.mean(proj, -1, keepdims=True)
     inv_std = lax.rsqrt(jnp.mean(centre * centre, -1, keepdims=True) + EPS_NORM)
     normed = centre * inv_std
-    upstream = grad_ref[...].astype(jnp.float32)
+    upstream = grad_ref[...].astype(f32)
     d_gain_ref[...] = jnp.sum(upstream * normed, 0, keepdims=True)
     scaled = upstream * gain_ref[...]
     d_proj = inv_std * (
@@ -171,49 +189,53 @@
         - jnp.mean(scaled, -1, keepdims=True)
         - normed * jnp.mean(scaled * normed, -1, keepdims=True)
     )
-    d_proj = d_proj.astype(jnp.bfloat16)
+    d_proj = d_proj.astype(b16)
     d_wproj_ref[...] = mxu(att_ref[...], d_proj, TN)
-    d_att_ref[...] = mxu(d_proj, w_proj_ref[...], NT).astype(jnp.bfloat16)
+    d_att_ref[...] = mxu(d_proj, w_proj_ref[...], NT).astype(b16)
     d_bias_ref[...] = jnp.zeros_like(d_bias_ref)
-    d_cos_ref[...] = jnp.zeros_like(d_cos_ref)
-
-    def backward(w, carry):
-        rows = pl.ds(pl.multiple_of(w * length, length), length)
-        for g in range(groups):
-            query, key, value = load(w, g, 0), load(w, g, 1), load(w, g, 2)
-            d_att = d_att_ref[rows, g * lanes : (g + 1) * lanes]
-            probs = probs_ref[w, g]
-            cosine = cos_ref[w, g]
-            tall = spread(key, head_dim, length)
-            d_probs = mxu(d_att, spread(value, head_dim, length), NT)
-            d_value = gather_heads(
-                mxu(probs.astype(jnp.bfloat16), d_att, TN), head_dim, length
-            )
-            d_scores = probs * (d_probs - mxu_fine(d_probs * probs, wide_ones, NN))
-            d_bias_ref[g] += d_scores
-            d_cos_ref[g] += d_scores * cosine
-            scaled_scores = d_scores * scale_ref[g]
-            query32, key32 = query.astype(jnp.float32), key.astype(jnp.float32)
-            query_sum = mxu_fine(jnp.square(query32), lane_ones, NN)
-            query_wide = lax.rsqrt(query_sum + 1.0)
-            query_inv = lax.rsqrt(mxu_fine(jnp.square(query32), lane_lane, NN) + 1.0)
-            key_inv = lax.rsqrt(mxu_fine(jnp.square(key32), lane_lane, NN) + 1.0)
-            d_unit_q = mxu_fine(scaled_scores * key_row_inv(tall), tall, NN)
-            d_unit_k = gather_heads(
-                mxu_fine(scaled_scores * query_wide, query, TN), head_dim, length
-            )
-            unit_q, unit_k = query32 * query_inv, key32 * key_inv
-            d_query = query_inv * (d_unit_q - unit_q * mxu_fine(unit_q * d_unit_q, lane_lane, NN))
-            d_key = key_inv * (d_unit_k - unit_k * mxu_fine(unit_k * d_unit_k, lane_lane, NN))
-            for part, grad in enumerate((d_query, d_key, d_value)):
-                d_qkv_ref[rows, part * depth + g * lanes : part * depth + (g + 1) * lanes] = (
-                    grad.astype(jnp.bfloat16)
-                )
-        return carry
-
-    lax.fori_loop(0, count, backward, 0)
+
+    for g in range(groups):
+
+        def backward(step, carry):
+            units = [step * BWD + k for k in range(BWD)]
+            grads = []
+            for w in units:
+                d_tall = tile_heads(load(d_att_ref, w, g, 0), head_dim, length)
+                d_probs = mxu(load(qkv_ref, w, g, 2), d_tall, NT)
+                d_value = mxu(probs_ref[w, g].astype(b16), d_tall, NN)
+                d_qkv_ref[
+                    pl.ds(pl.multiple_of(w * length, length), length),
+                    2 * depth + g * lanes : 2 * depth + (g + 1) * lanes,
+                ] = d_value.astype(b16)
+                grads.append(d_probs)
+            total = d_bias_ref[g]
+            for w, d_probs in zip(units, grads):
+                rows = pl.ds(pl.multiple_of(w * length, length), length)
+                probs = probs_ref[w, g]
+                d_scores = probs * (d_probs - jnp.sum(d_probs * probs, 0, keepdims=True))
+                total = total + d_scores
+                high, low = split(d_scores * kinv_ref[g, rows, :] * qrow_ref[w, g])
+                both = jnp.concatenate([high, low], 0)
+                query, key = load(qkv_ref, w, g, 0), load(qkv_ref, w, g, 1)
+                pair = mxu(both, tile_heads(query, head_dim, length), NN)
+                raw_k_ref[rows, :] = pair[:length] + pair[length:]
+                tall = mxu(both, jnp.concatenate([key, key], 0), TN)
+                raw_q_ref[rows, :] = gather_heads(tall, head_dim, length)
+            d_bias_ref[g] = total
+            return carry
+
+        lax.fori_loop(0, count // BWD, backward, 0)
+        for part, ref in enumerate((raw_q_ref, raw_k_ref)):
+            place = slice(part * depth + g * lanes, part * depth + (g + 1) * lanes)
+            value, grad = qkv_ref[:, place].astype(f32), ref[...]
+            along = value * grad
+            if part == 0:
+                d_cos_ref[g] = jnp.sum(along, 0, keepdims=True)
+            d_qkv_ref[:, place] = (
+                grad - value * norm_ref[part, g] * mxu_fine(along, lane_lane, NN)
+            ).astype(b16)
     d_wqkv_ref[...] = mxu(flat_ref[...], d_qkv_ref[...], TN)
-    d_flat_ref[...] = mxu(d_qkv_ref[...], w_qkv_ref[...], NT).astype(jnp.bfloat16)
+    d_flat_ref[...] = mxu(d_qkv_ref[...], w_qkv_ref[...], NT).astype(b16)
 
 
 def offset_onehot(window):
@@ -243,14 +265,14 @@
     tokens = flat.shape[0]
     count = tokens // length
     scale = jnp.exp(jnp.minimum(logit_scale, SCALE_CAP))
-    scale_rows = jnp.repeat(scale.reshape(groups, GROUP), length, 1).reshape(groups, 1, wide)
+    scale_rows = jnp.pad(scale, (0, -heads % 16)).reshape(-1, 1) * jnp.ones((1, 128), jnp.float32)
     sigma = jax.nn.sigmoid(table_logits)
     entries = table_logits.shape[1]
     hot = offset_onehot(window)[None, :] == jnp.arange(entries, dtype=jnp.int32)[:, None]
     hot = hot.astype(jnp.bfloat16)
     parts = jnp.dot(three_parts(sigma * BIAS_RANGE), hot, preferred_element_type=jnp.float32)
     rel_bias = jnp.sum(parts.reshape(3, heads, -1), 0).reshape(groups, GROUP, length, length)
-    rel_bias = rel_bias.transpose(0, 2, 1, 3).reshape(groups, length, wide)
+    rel_bias = rel_bias.transpose(0, 3, 1, 2).reshape(groups, length, wide)
     f32, b16 = jnp.float32, jnp.bfloat16
     d_flat, d_wqkv, d_wproj, d_bias, d_cos, d_gain = pl.pallas_call(
         functools.partial(local_kernel, cols // window, height, width, window),
@@ -259,7 +281,7 @@
             jax.ShapeDtypeStruct((depth, 3 * depth), f32),
             jax.ShapeDtypeStruct((depth, depth), f32),
             jax.ShapeDtypeStruct((groups, length, wide), f32),
-            jax.ShapeDtypeStruct((groups, length, wide), f32),
+            jax.ShapeDtypeStruct((groups, 1, depth // groups), f32),
             jax.ShapeDtypeStruct((1, depth), f32),
         ],
         in_specs=[VMEM] * 7,
@@ -270,7 +292,12 @@
             pltpu.VMEM((tokens, depth), b16),
             pltpu.VMEM((tokens, 3 * depth), b16),
             pltpu.VMEM((count, groups, length, wide), f32),
-            pltpu.VMEM((count, groups, length, wide), f32),
+            pltpu.VMEM((groups, tokens, wide), f32),
+            pltpu.VMEM((count, groups, 1, wide), f32),
+            pltpu.VMEM((4, groups, length, wide), f32),
+            pltpu.VMEM((tokens, depth // groups), f32),
+            pltpu.VMEM((tokens, depth // groups), f32),
+            pltpu.VMEM((2, groups, tokens, depth // groups), f32),
         ],
         compiler_params=pltpu.CompilerParams(vmem_limit_bytes=48 * 2**20),
         cost_estimate=pl.CostEstimate(
@@ -278,13 +305,12 @@
         ),
         name="local_grads",
     )(flat, grad_flat, w_qkv, w_proj, rel_bias, scale_rows, gain.reshape(1, depth))
-    heads_bias = d_bias.reshape(groups, length, GROUP, length).transpose(0, 2, 1, 3)
+    heads_bias = d_bias.reshape(groups, length, GROUP, length).transpose(0, 2, 3, 1)
     heads_bias = heads_bias.reshape(heads, length * length)
     sums = lax.dot_general(three_parts(heads_bias), hot, NT, preferred_element_type=jnp.float32)
     d_table = jnp.sum(sums.reshape(3, heads, entries), 0) * (BIAS_RANGE * sigma * (1.0 - sigma))
     live = (logit_scale < SCALE_CAP).astype(jnp.float32)
-    d_scale = jnp.sum(d_cos.reshape(groups, length, GROUP, length), (1, 3)).reshape(heads)
-    d_scale = d_scale * scale * live
+    d_scale = jnp.sum(d_cos.reshape(heads, depth // heads), 1) * live
     d_block = from_windows(d_flat.reshape(images, count, length, depth), images, rows, cols, window)
     return (d_block, (d_wqkv, d_wproj, d_table, d_scale, d_gain.reshape(depth)))
 

time: 87.9 us -> 70.7 us (0.80)
  Pallas kernels: 59.1 us -> 40.3 us
  other arithmetic: 3.52 us -> 5.88 us
  local copies, waits for them, and re-layouts: 8.47 us -> 6.93 us
    pallas_call x1, Pallas kernels: 29.8 us -> 10.7 us  [local_grads(): pl.pallas_call(functools.partial(local_kernel, cols // window, height, wi...]
    reshape x5 -> x3, local copies, waits for them, and re-layouts: 1.41 us -> 0.39 us  [the longest x1 0.16 us: local_grads(): d_bias.reshape(groups, length, GROUP, length).transpose(0, 2, 3, 1)]
    reshape x1, local copies, waits for them, and re-layouts: 1.15 us -> 0.14 us  [local_grads(): heads_bias = heads_bias.reshape(heads, length * length)]
    unnamed x33 -> x29, local copies, waits for them, and re-layouts: 3.85 us -> 4.15 us
  transfers between devices with their start and end apart: 4 -> 4, of which waited for: 2 -> 2; matrix products, arithmetic and copies ran while one was open for 11% -> 13% of each run, Pallas kernels for 34% -> 42%
where the time goes in v1:
time: 70.7 us; the launch traced here: 70.1 us
  Pallas kernels  40.3 us (57%)
  starting transfers between devices  8.1 us (11%)
  local copies, waits for them, and re-layouts  6.93 us (10%)
  other arithmetic  5.88 us (8%)
  waiting for transfers between devices  5.02 us (7%)
  matrix products  2.98 us (4%)
  between operations  0.95 us (1%)
    pallas_call x1, Pallas kernels, reduce_all(): pl.pallas_call(functools.partial(reduce_kernel, (size_h, size_w)), out_sh...  29.6 us
    pallas_call x1, Pallas kernels, local_grads(): pl.pallas_call(functools.partial(local_kernel, cols // window, height, wi...  10.7 us
    ppermute x4, starting transfers between devices, from_behind(): return lax.ppermute(block, axis, route)  8.1 us
    ppermute x4, waiting for transfers between devices, from_behind(): return lax.ppermute(block, axis, route)  5.02 us
    unnamed x29, local copies, waits for them, and re-layouts  4.15 us
    convert_element_type x1, other arithmetic, shards(): (cotangent.astype(jnp.float32) + back.astype(jnp.float32)).astype(jnp.bfl...  1.68 us
    dot_general x1, matrix products, local_grads(): lax.dot_general(three_parts(heads_bias), hot, NT, preferred_element_type=...  1.52 us
    dot_general x1, matrix products, local_grads(): jnp.dot(three_parts(sigma * BIAS_RANGE), hot, preferred_element_type=jnp....  1.46 us
  transfers between devices with their start and end apart: 4, of which 2 were waited for; matrix products, arithmetic and copies ran while one was open for 13% of the time, Pallas kernels for 42%

profile of v1, /device:TPU:0, one launch (start us, length us, event | category | flops | bytes accessed | tf_op | source)
XLA Modules:
  0.0 70.1 jit_solution(9342312000034557929)
XLA Ops:
  0.7 1.0 %pad_maximum_fusion.2 = bf16[2,1,4,32,384]{4,3,2,1,0:T(8,128)(2,1)S(1)} fusion(bf16[1,1,16,32,384]{4,3,2,1,0:T(8,128)(2,1)} %bitcast.34, bf16[1,1,16,32,384]{4,3,2,1,0:T(8,128)(2,1)} %bitcast.40), kind=kLoop, calls=%fused_computation.26 | loop fusion | flops 98304 | bytes 983040 | tf_op jit(solution)/shard_map/stack | solution.py:507
  1.6 4.6 %collective-permute-start = (bf16[2,1,4,32,384]{4,3,2,1,0:T(8,128)(2,1)S(1)}, bf16[2,1,4,32,384]{4,3,2,1,0:T(8,128)(2,1)S(1)}, u32[]{:S(2)}, u32[]{:S(2)}) collective-permute-start(bf16[2,1,4,32,384]{4,3,2,1,0:T(8,128)(2,1)S(1)} %pad_maximum_fusion.2), channel_id=1, source_target_pairs={{4,0},{8,4},{12,8},{16,12},{20,16},{24,20},{28,24},{0,28},{5,1},{9... | collective-permute-start | bytes 589832 | tf_op jit(solution)/shard_map/ppermute | solution.py:25
  6.2 0.7 %reduce-precision_convert_fusion.3 = (bf16[12,225]{1,0:T(8,128)(2,1)S(1)}, bf16[12,225]{1,0:T(8,128)(2,1)S(1)}, bf16[12,225]{1,0:T(8,128)(2,1)S(1)}) fusion(f32[12,225]{1,0:T(8,128)} %param.12), kind=kLoop, calls=%fused_computation.32 | loop fusion | flops 29700 | bytes 27000 | tf_op jit(solution)/shard_map/convert.3
  6.9 1.5 %fusion.1 = f32[36,4096]{1,0:T(8,128)S(1)} fusion(s32[4096]{0:T(1024)} %constant.13.clone, bf16[12,225]{1,0:T(8,128)(2,1)S(1)} %get-tuple-element.42, bf16[12,225]{1,0:T(8,128)(2,1)S(1)} %get-tuple-element.43, bf16[12,225]{1,0:T(8,128)(2,1)S(1)} %get-tuple-element.41), kind=kOutput, calls=%fused_computation.2 | convolution fusion | flops 67325400 | bytes 622408 | tf_op jit(solution)/shard_map/dot_general | solution.py:273
  8.6 0.2 reshape.80
  8.8 0.1 copy.26.bias_ref
  8.9 0.5 copy-done.7
  9.4 0.1 copy-done.9
  9.7 1.6 %collective-permute-start.1 = (bf16[2,1,16,4,384]{4,3,2,1,0:T(4,128)(2,1)S(1)}, bf16[2,1,16,4,384]{4,3,2,1,0:T(4,128)(2,1)S(1)}, u32[]{:S(2)}, u32[]{:S(2)}) collective-permute-start(bf16[2,1,16,4,384]{4,3,2,1,0:T(4,128)(2,1)S(1)} %pad_maximum_fusion.4), channel_id=1, source_target_pairs={{2,0},{0,2},{3,1},{1,3},{6,4},{4,6},{7,5},{5,7},{10,8},{8,10},{11,... | collective-permute-start | bytes 294920 | tf_op jit(solution)/shard_map/ppermute | solution.py:25
  11.3 0.2 slice_maximum_fusion
  11.6 2.8 %collective-permute-done.1 = bf16[2,1,16,4,384]{4,3,2,1,0:T(4,128)(2,1)S(1)} collective-permute-done((bf16[2,1,16,4,384]{4,3,2,1,0:T(4,128)(2,1)S(1)}, bf16[2,1,16,4,384]{4,3,2,1,0:T(4,128)(2,1)S(1)}, u32[]{:S(2)}, u32[]{:S(2)}) %collective-permute-start.1) | collective-permute-done | bytes 98336 | tf_op jit(solution)/shard_map/ppermute | solution.py:25
  14.4 0.1 pad_maximum_fusion.1
  14.7 10.7 %local_grads.1 = (bf16[512,384]{1,0:T(8,128)(2,1)S(1)}, f32[384,1152]{1,0:T(8,128)S(1)}, f32[384,384]{1,0:T(8,128)S(1)}, f32[3,64,256]{2,1,0:T(8,128)S(1)}, f32[...) custom-call(bf16[512,384]{1,0:T(8,128)(2,1)S(1)} %bitcast.28, bf16[512,384]{1,0:T(8,128)(2,1)S(1)} %bitcast.27, ...), custom_call_target="tpu_custom_call" | custom-call | flops 4000000000 | bytes 8000000 | tf_op jit(solution)/shard_map/local_grads/pallas_call | solution.py:277
  25.6 0.1 reduce_sum.29
  25.7 0.1 select_maximum_fusion.1
  25.8 0.7 slice.62
  26.5 1.5 %collective-permute-start.2 = (bf16[1,16,4,384]{3,2,1,0:T(4,128)(2,1)}, bf16[1,16,4,384]{3,2,1,0:T(4,128)(2,1)}, u32[]{:S(2)}, u32[]{:S(2)}) collective-permute-start(bf16[1,16,4,384]{3,2,1,0:T(4,128)(2,1)} %slice.62), channel_id=1, source_target_pairs={{2,0},{0,2},{3,1},{1,3},{6,4},{4,6},{7,5},{5,7},{10,8},{8,10},{11,... | collective-permute-start | bytes 147464 | tf_op jit(solution)/shard_map/ppermute | solution.py:25
  28.0 0.2 copy.27
  28.2 0.1 reshape.85
  28.4 1.5 %fusion = f32[36,225]{1,0:T(8,128)S(1)} fusion(s32[4096]{0:T(1024)} %constant.13.clone, bf16[12,4096]{1,0:T(8,128)(2,1)S(1)} %get-tuple-element.39, bf16[12,4096]{1,0:T(8,128)(2,1)S(1)} %get-tuple-element.40, bf16[12,4096]{1,0:T(8,128)(2,1)S(1)} %get-tuple-element.38), kind=kOutput, calls=%fused_computation.1 | convolution fusion | flops 68161536 | bytes 343696 | tf_op jit(solution)/shard_map/dot_general | solution.py:310
  30.0 0.8 %multiply_multiply_fusion = f32[12,225]{1,0:T(8,128)S(1)} fusion(f32[12,225]{1,0:T(8,128)S(1)} %reduce_sum.28, f32[12,225]{1,0:T(8,128)} %param.12), kind=kLoop, calls=%fused_computation.41 | loop fusion | flops 18900 | bytes 32400 | tf_op jit(solution)/shard_map/mul | solution.py:311
  30.8 29.6 %reduce_all.1 = (f32[384,576]{1,0:T(8,128)S(1)}, f32[384,192]{1,0:T(8,128)S(1)}, f32[16,256]{1,0:T(8,128)S(1)}) custom-call(f32[384,1152]{1,0:T(8,128)S(1)} %get-tuple-element.16.wqkv_ref, f32[384,384]{1,0:T(8,128)S(1)} %get-tuple-element.17.wproj_ref, f32[16,256]{1,0:T(8,128)S(1)} %pad.19.small_ref), custom_call_target="tpu_custom_call" | custom-call | tf_op jit(solution)/shard_map/reduce_all/pallas_call | solution.py:445
  60.3 0.7 %copy-done = f32[384,192]{1,0:T(8,128)} copy-done((f32[384,192]{1,0:T(8,128)}, f32[384,192]{1,0:T(8,128)S(1)}, u32[]{:S(2)}) %copy-start) | copy-done | bytes 294936
  61.1 0.8 %pad_maximum_fusion.3 = bf16[1,4,32,384]{3,2,1,0:T(8,128)(2,1)S(1)} fusion(bf16[1,16,28,384]{3,2,1,0:T(8,128)(2,1)S(1)} %bitcast.32, bf16[1,16,4,384]{3,2,1,0:T(4,128)(2,1)} %collective-permute-done.2), kind=kLoop, calls=%fused_computation.27 | loop fusion | flops 196608 | bytes 491520 | tf_op jit(solution)/shard_map/slice | solution.py:520
  62.0 0.4 collective-permute-start.3
  62.4 0.5 slice.54
  62.9 0.6 slice.55
  63.6 1.2 %copy.24 = f32[384,576]{0,1:T(8,128)} copy(f32[384,576]{1,0:T(8,128)S(1)} %get-tuple-element.31) | data formatting | bytes 1769472
  64.8 0.9 %copy.25 = f32[384,192]{0,1:T(8,128)} copy(f32[384,192]{1,0:T(8,128)S(1)} %copy-done.1) | data formatting | bytes 589824
  65.6 2.2 %collective-permute-done.3 = bf16[1,4,32,384]{3,2,1,0:T(8,128)(2,1)S(1)} collective-permute-done((bf16[1,4,32,384]{3,2,1,0:T(8,128)(2,1)S(1)}, bf16[1,4,32,384]{3,2,1,0:T(8,128)(2,1)S(1)}, u32[]{:S(2)}, u32[]{:S(2)}) %collective-permute-start.3) | collective-permute-done | bytes 98336 | tf_op jit(solution)/shard_map/ppermute | solution.py:25
  67.9 1.7 %add_convert_fusion = bf16[1,16,32,384]{3,2,1,0:T(8,128)(2,1)} fusion(bf16[1,16,32,384]{3,2,1,0:T(8,128)(2,1)S(1)} %copy-done.8, bf16[1,16,28,384]{3,2,1,0:T(8,128)(2,1)S(1)} %bitcast.33, bf16[1,16,4,384]{3,2,1,0:T(4,128)(2,1)} %collective-permute-done.2, bf16[1,4,32,384]{3,2,1,0:T(8,128)(2,1)S(1)} %collective-permute-done.3), kind=kLoop, calls=%fused_computation.10 | loop fusion | flops 1769472 | bytes 1277952 | tf_op jit(solution)/shard_map/convert_element_type | solution.py:536
  69.5 0.6 copy.30
  (46 shorter events, 0.7 us)
Async XLA Ops:
  0.6 7.8 %copy-start.11 = (f32[12]{0:T(128)S(1)}, f32[12]{0:T(128)}, u32[]{:S(2)}) copy-start(f32[12]{0:T(128)} %param.13) | copy-start | bytes 148
  0.6 7.8 %copy-start.10 = (f32[384]{0:T(512)S(1)}, f32[384]{0:T(512)}, u32[]{:S(2)}) copy-start(f32[384]{0:T(512)} %param.14) | copy-start | bytes 4612
  1.6 8.0 %collective-permute-start = (bf16[2,1,4,32,384]{4,3,2,1,0:T(8,128)(2,1)S(1)}, bf16[2,1,4,32,384]{4,3,2,1,0:T(8,128)(2,1)S(1)}, u32[]{:S(2)}, u32[]{:S(2)}) collective-permute-start(bf16[2,1,4,32,384]{4,3,2,1,0:T(8,128)(2,1)S(1)} %pad_maximum_fusion.2), channel_id=1, source_target_pairs={{4,0},{8,4},{12,8},{16,12},{20,16},{24,20},{28,24},{0,28},{5,1},{9... | collective-permute-start | bytes 589832 | tf_op jit(solution)/shard_map/ppermute | solution.py:25
  8.5 1.0 %copy-start.7 = (bf16[1,16,32,384]{3,2,1,0:T(8,128)(2,1)S(1)}, bf16[1,16,32,384]{3,2,1,0:T(8,128)(2,1)}, u32[]{:S(2)}) copy-start(bf16[1,16,32,384]{3,2,1,0:T(8,128)(2,1)} %param.9) | copy-start | bytes 1179652
  8.5 1.1 %copy-start.9 = (bf16[1,16,32,384]{3,2,1,0:T(8,128)(2,1)S(1)}, bf16[1,16,32,384]{3,2,1,0:T(8,128)(2,1)}, u32[]{:S(2)}) copy-start(bf16[1,16,32,384]{3,2,1,0:T(8,128)(2,1)} %param.8) | copy-start | bytes 1179652
  9.7 4.7 %collective-permute-start.1 = (bf16[2,1,16,4,384]{4,3,2,1,0:T(4,128)(2,1)S(1)}, bf16[2,1,16,4,384]{4,3,2,1,0:T(4,128)(2,1)S(1)}, u32[]{:S(2)}, u32[]{:S(2)}) collective-permute-start(bf16[2,1,16,4,384]{4,3,2,1,0:T(4,128)(2,1)S(1)} %pad_maximum_fusion.4), channel_id=1, source_target_pairs={{2,0},{0,2},{3,1},{1,3},{6,4},{4,6},{7,5},{5,7},{10,8},{8,10},{11,... | collective-permute-start | bytes 294920 | tf_op jit(solution)/shard_map/ppermute | solution.py:25
  11.5 3.2 %copy-start.2 = (bf16[384,1152]{1,0:T(8,128)(2,1)S(1)}, bf16[384,1152]{1,0:T(8,128)(2,1)}, u32[]{:S(2)}) copy-start(bf16[384,1152]{1,0:T(8,128)(2,1)} %w_qkv_ref.1) | copy-start | bytes 2654212
  11.5 3.2 %copy-start.3 = (bf16[384,384]{1,0:T(8,128)(2,1)S(1)}, bf16[384,384]{1,0:T(8,128)(2,1)}, u32[]{:S(2)}) copy-start(bf16[384,384]{1,0:T(8,128)(2,1)} %w_proj_ref.1) | copy-start | bytes 884740
  25.5 4.4 %copy-start.4 = (bf16[1,2,8,4,8,384]{5,4,3,2,1,0:T(8,128)(2,1)}, bf16[1,2,8,4,8,384]{5,4,3,2,1,0:T(8,128)(2,1)S(1)}, u32[]{:S(2)}) copy-start(bf16[1,2,8,4,8,384]{5,4,3,2,1,0:T(8,128)(2,1)S(1)} %copy.22) | copy-start | bytes 1179652
  26.5 34.6 %collective-permute-start.2 = (bf16[1,16,4,384]{3,2,1,0:T(4,128)(2,1)}, bf16[1,16,4,384]{3,2,1,0:T(4,128)(2,1)}, u32[]{:S(2)}, u32[]{:S(2)}) collective-permute-start(bf16[1,16,4,384]{3,2,1,0:T(4,128)(2,1)} %slice.62), channel_id=1, source_target_pairs={{2,0},{0,2},{3,1},{1,3},{6,4},{4,6},{7,5},{5,7},{10,8},{8,10},{11,... | collective-permute-start | bytes 147464 | tf_op jit(solution)/shard_map/ppermute | solution.py:25
  29.9 31.2 %copy-start.5 = (bf16[1,2,8,4,8,384]{5,4,3,2,1,0:T(8,128)(2,1)S(1)}, bf16[1,2,8,4,8,384]{5,4,3,2,1,0:T(8,128)(2,1)}, u32[]{:S(2)}) copy-start(bf16[1,2,8,4,8,384]{5,4,3,2,1,0:T(8,128)(2,1)} %copy-done.4) | copy-start | bytes 1179652
  60.3 0.8 %copy-start = (f32[384,192]{1,0:T(8,128)}, f32[384,192]{1,0:T(8,128)S(1)}, u32[]{:S(2)}) copy-start(f32[384,192]{1,0:T(8,128)S(1)} %get-tuple-element.32) | copy-start | bytes 884740
  61.1 6.8 %copy-start.6 = (bf16[1,2,8,4,8,384]{5,4,3,2,1,0:T(8,128)(2,1)S(1)}, bf16[1,2,8,4,8,384]{5,4,3,2,1,0:T(8,128)(2,1)}, u32[]{:S(2)}) copy-start(bf16[1,2,8,4,8,384]{5,4,3,2,1,0:T(8,128)(2,1)} %copy-done.4) | copy-start | bytes 1179652
  61.1 6.8 %copy-start.8 = (bf16[1,16,32,384]{3,2,1,0:T(8,128)(2,1)S(1)}, bf16[1,16,32,384]{3,2,1,0:T(8,128)(2,1)}, u32[]{:S(2)}) copy-start(bf16[1,16,32,384]{3,2,1,0:T(8,128)(2,1)} %param.9) | copy-start | bytes 1179652
  61.1 3.7 %copy-start.1 = (f32[384,192]{1,0:T(8,128)S(1)}, f32[384,192]{1,0:T(8,128)}, u32[]{:S(2)}) copy-start(f32[384,192]{1,0:T(8,128)} %copy-done) | copy-start | bytes 884740
  62.0 5.9 %collective-permute-start.3 = (bf16[1,4,32,384]{3,2,1,0:T(8,128)(2,1)S(1)}, bf16[1,4,32,384]{3,2,1,0:T(8,128)(2,1)S(1)}, u32[]{:S(2)}, u32[]{:S(2)}) collective-permute-start(bf16[1,4,32,384]{3,2,1,0:T(8,128)(2,1)S(1)} %pad_maximum_fusion.3), channel_id=1, source_target_pairs={{28,0},{0,4},{4,8},{8,12},{12,16},{16,20},{20,24},{24,28},{29,1},{... | collective-permute-start | bytes 294920 | tf_op jit(solution)/shard_map/ppermute | solution.py:25

commit v2 on v1

--- a/solution.py
+++ b/solution.py
@@ -47,6 +47,8 @@
 FWD = 2
 BWD = 4
 LOG2E = math.log2(math.e)
+VMEM_LIMIT = 40 * 2**20
+FINISH_LIMIT = 4 * 2**20
 MESH = pl.DeviceIdType.MESH
 VMEM = pl.BlockSpec(memory_space=pltpu.VMEM)
 NN = (((1,), (0,)), ((), ()))
@@ -74,7 +76,7 @@
     return (row == col).astype(jnp.bfloat16)
 
 
-def tile_heads(value, width, reps):
+def tile_heads(value, width):
     lane = lax.broadcasted_iota(jnp.int32, (1, value.shape[1]), 1) % (GROUP * width) // width
     rows = []
     for head in range(GROUP):
@@ -160,7 +162,7 @@
         scores = []
         for w, g in units:
             query, key = load(qkv_ref, w, g, 0), load(qkv_ref, w, g, 1)
-            raw = mxu(key, tile_heads(query, head_dim, length), NT)
+            raw = mxu(key, tile_heads(query, head_dim), NT)
             last_row = (row_base + w // grid_cols * window) // (height - window)
             last_col = (col_base + w % grid_cols * window) // (width - window)
             kinv = kinv_ref[g, pl.ds(pl.multiple_of(w * length, length), length), :]
@@ -200,7 +202,7 @@
             units = [step * BWD + k for k in range(BWD)]
             grads = []
             for w in units:
-                d_tall = tile_heads(load(d_att_ref, w, g, 0), head_dim, length)
+                d_tall = tile_heads(load(d_att_ref, w, g, 0), head_dim)
                 d_probs = mxu(load(qkv_ref, w, g, 2), d_tall, NT)
                 d_value = mxu(probs_ref[w, g].astype(b16), d_tall, NN)
                 d_qkv_ref[
@@ -217,7 +219,7 @@
                 high, low = split(d_scores * kinv_ref[g, rows, :] * qrow_ref[w, g])
                 both = jnp.concatenate([high, low], 0)
                 query, key = load(qkv_ref, w, g, 0), load(qkv_ref, w, g, 1)
-                pair = mxu(both, tile_heads(query, head_dim, length), NN)
+                pair = mxu(both, tile_heads(query, head_dim), NN)
                 raw_k_ref[rows, :] = pair[:length] + pair[length:]
                 tall = mxu(both, jnp.concatenate([key, key], 0), TN)
                 raw_q_ref[rows, :] = gather_heads(tall, head_dim, length)
@@ -315,11 +317,98 @@
     return (d_block, (d_wqkv, d_wproj, d_table, d_scale, d_gain.reshape(depth)))
 
 
-def reduce_kernel(
-    shape, wqkv_ref, wproj_ref, small_ref, qkv_out, proj_out, small_out,
-    core_send, core_get, image_keep, image_send, image_get, near_send, near_get, own, whole, core_all,
-    small_core, small_image, small_a, small_b, small_near,
-    core_sems, image_sems, near_sems, all_sems, last_sems, tiny_sems,
+def half_turn(value, axis):
+    return pltpu.roll(value, value.shape[axis] // 2, axis)
+
+
+def exp_fine(value):
+    whole = jnp.floor(value * LOG2E + 0.5)
+    rest = value - whole * 0.693359375 + whole * 2.12194440e-4
+    total = jnp.ones_like(rest)
+    for k in range(8, 0, -1):
+        total = 1.0 + total * rest * (1.0 / k)
+    return total * jnp.exp2(whole)
+
+
+def inverse(value):
+    guess = 1.0 / value
+    return guess * (2.0 - value * guess)
+
+
+def place_of(index, window):
+    return index // window * (2 * window - 1) + index % window
+
+
+def expand_bias(table, length, window, groups, out_ref):
+    span = table.shape[1]
+    f32, b16 = jnp.float32, jnp.bfloat16
+    heads = groups * GROUP
+    base = jnp.concatenate([jnp.broadcast_to(table[h : h + 1], (window, span)) for h in range(heads)], 0)
+    sub = lax.broadcasted_iota(jnp.int32, base.shape, 0) % window
+    bit = 1
+    while bit < window:
+        base = jnp.where(sub // bit % 2 == 1, pltpu.roll(base, bit, 1), base)
+        bit *= 2
+    top = place_of(length - 1, window)
+    turned = [
+        pltpu.roll(base, (span - top + (2 * window - 1) * r) % span, 1)[:, : span // 2] for r in range(window)
+    ]
+    wide = GROUP * length
+    row = lax.broadcasted_iota(jnp.int32, (span, wide), 0) % (span // 2)
+    col = lax.broadcasted_iota(jnp.int32, (span, wide), 1)
+    hit = row == place_of(col % length, window)
+    for g in range(groups):
+        total = jnp.zeros((length, wide), f32)
+        for k in range(GROUP):
+            h = g * GROUP + k
+            block = jnp.concatenate([t[h * window : (h + 1) * window] for t in turned], 0)
+            pair = jnp.concatenate(split(block), 1)
+            total = total + mxu(pair, (hit & (col // length == k)).astype(b16), NN)
+        out_ref[0, g] = total
+
+
+def fold_bias(grads, length, window, span):
+    f32, b16 = jnp.float32, jnp.bfloat16
+    wide = GROUP * length
+    row = lax.broadcasted_iota(jnp.int32, (wide, span // 2), 0)
+    col = lax.broadcasted_iota(jnp.int32, (wide, span // 2), 1)
+    hit = col == place_of(row % length, window)
+    both = jnp.concatenate([half for grad in grads for half in split(grad)], 0)
+    by_head = [None] * (len(grads) * GROUP)
+    for k in range(GROUP):
+        pairs = mxu(both, (hit & (row // length == k)).astype(b16), NN)
+        for g in range(len(grads)):
+            pair = pairs[2 * g * length : (2 * g + 2) * length]
+            block = pair[:length] + pair[length:]
+            by_head[g * GROUP + k] = jnp.concatenate([block, jnp.zeros_like(block)], 1)
+    parts = [
+        jnp.concatenate([block[r * window : (r + 1) * window] for block in by_head], 0) for r in range(window)
+    ]
+    step = 2 * window - 1
+    while len(parts) > 1:
+        parts = [pltpu.roll(parts[i], step, 1) + parts[i + 1] for i in range(0, len(parts), 2)]
+        step *= 2
+    total = parts[0]
+    sub = window - 1 - lax.broadcasted_iota(jnp.int32, total.shape, 0) % window
+    bit = 1
+    while bit < window:
+        total = jnp.where(sub // bit % 2 == 1, pltpu.roll(total, bit, 1), total)
+        bit *= 2
+    return [jnp.sum(total[k * window : (k + 1) * window], 0, keepdims=True) for k in range(len(by_head))]
+
+
+def whole_kernel(
+    shape, height, width, window,
+    tokens_ref, cot_ref, w_qkv_hbm, w_proj_hbm, table_hbm, gain_hbm, scale_ref,
+    d_tok_ref, wq_out, wp_out, table_out, scale_out, gain_out,
+    tok, cot, w_qkv_ref, w_proj_ref, table_in, gain_ref, table_ref, local_sems,
+    col_send, row_get, col_get, diag_get, halo_sems,
+    flat_ref, grad_ref, d_flat_ref,
+    qkv_ref, att_ref, d_att_ref, d_qkv_ref, probs_ref, kinv_ref, qrow_ref, masked_ref, raw_q_ref, raw_k_ref,
+    norm_ref, d_bias_ref, p_mid, product_ref,
+    row_back, col_back, row_back_get, col_back_get, diag_back_get, back_sems,
+    small, small_core, small_a, small_image, small_b, small_near, tiny_sems,
+    *chunk_refs,
 ):
     size_h, size_w = shape
     chips = size_h // 2
@@ -328,27 +417,32 @@
     core = ha % 2
     me = wa * chips + ha // 2
     partner = (ha + 1 - 2 * core, wa, ba)
-    image = (ha, wa, 1 - ba)
+    image, side, corner = (ha, wa, 1 - ba), (ha, 1 - wa, ba), (ha, 1 - wa, 1 - ba)
+    above, below = lax.rem(ha + size_h - 1, size_h), lax.rem(ha + 1, size_h)
+    left, right = lax.rem(wa + size_w - 1, size_w), lax.rem(wa + 1, size_w)
+    f32, b16 = jnp.float32, jnp.bfloat16
 
     def peer(step):
         other = lax.rem(me + step, peers)
         return other, (other % chips * 2 + core, other // chips, ba)
 
+    loads = []
+    for k, (src, dst) in enumerate(
+        (
+            (tokens_ref.at[0], tok), (cot_ref.at[0], cot), (w_qkv_hbm, w_qkv_ref), (w_proj_hbm, w_proj_ref),
+            (table_hbm, table_in), (gain_hbm, gain_ref),
+        )
+    ):
+        copy = pltpu.make_async_copy(src, dst, local_sems.at[k])
+        copy.start()
+        loads.append(copy)
+    targets = [
+        (above, wa, ba), (below, wa, ba), (ha, left, ba), (ha, right, ba), (above, left, ba), (below, right, ba),
+        partner, image, corner,
+    ] + [peer(step)[1] for step in range(1, peers)]
     barrier = pltpu.get_barrier_semaphore()
-    pl.semaphore_signal(barrier, inc=1, device_id=partner, device_id_type=MESH)
-    pl.semaphore_signal(barrier, inc=1, device_id=image, device_id_type=MESH)
-    for step in range(1, peers):
-        pl.semaphore_signal(barrier, inc=1, device_id=peer(step)[1], device_id_type=MESH)
-
-    depth = wqkv_ref.shape[0]
-    half = depth // 2
-    q_half, p_half = wqkv_ref.shape[1] // 2, wproj_ref.shape[1] // 2
-    f32, b16 = jnp.float32, jnp.bfloat16
-    mine = pl.ds(pl.multiple_of(core * half, 16), half)
-    theirs = pl.ds(pl.multiple_of((1 - core) * half, 16), half)
-    core_send[:, : 2 * q_half] = wqkv_ref[theirs, :].astype(b16)
-    core_send[:, 2 * q_half :] = wproj_ref[theirs, :].astype(b16)
-    pl.semaphore_wait(barrier, peers + 1)
+    for device in targets:
+        pl.semaphore_signal(barrier, inc=1, device_id=device, device_id_type=MESH)
 
     def start(src, dst, sems, device):
         copy = pltpu.make_async_remote_copy(
@@ -358,149 +452,516 @@
         copy.start()
         return copy
 
-    big = start(core_send, core_get, core_sems, partner)
-    tiny = start(small_ref, small_core, tiny_sems.at[0], partner)
+    rows, cols, depth = tok.shape
+    cut = window // 2
+    length = window * window
+    across = cols // window
+    count = rows // window * across
+    tokens = count * length
+    groups = qrow_ref.shape[1]
+    lanes = depth // groups
+    head_dim = lanes // GROUP
+    wide = GROUP * length
+    low_sub = lax.broadcasted_iota(jnp.int32, (window, depth), 0) < cut
+
+    for a, ref in enumerate((tok, cot)):
+        loads[a].wait()
+        for j in range(rows // 2):
+            first = ref[2 * j, :window, :].astype(f32)
+            second = ref[2 * j + 1, :window, :].astype(f32)
+            col_send[a, j] = jnp.where(low_sub, first, half_turn(second, 0)).astype(b16)
+    pl.semaphore_wait(barrier, len(targets))
+    halos = []
+    for a, ref in enumerate((tok, cot)):
+        halos.append(start(ref.at[pl.ds(0, cut)], row_get.at[a], halo_sems.at[a, 0], (above, wa, ba)))
+        halos.append(start(col_send.at[a], col_get.at[a], halo_sems.at[a, 1], (ha, left, ba)))
+        halos.append(
+            start(col_send.at[a, pl.ds(0, cut // 2)], diag_get.at[a], halo_sems.at[a, 2], (above, left, ba))
+        )
+
+    loads[4].wait()
+    loads[5].wait()
+    heads = groups * GROUP
+    entries = table_in.shape[1]
+    table_ref[...] = jnp.zeros_like(table_ref)
+    table_ref[:heads, :entries] = table_in[...]
+    sigma = inverse(1.0 + exp_fine(-table_ref[...]))
+    head_rows, span = table_ref.shape
+    spot = lax.broadcasted_iota(jnp.int32, (head_rows, 128), 0)
+    logits = jnp.zeros((head_rows, 128), f32)
+    for h in range(heads):
+        logits = jnp.where(spot == h, scale_ref[h], logits)
+    scale = exp_fine(jnp.minimum(logits, SCALE_CAP))
+    expand_bias(sigma * (BIAS_RANGE * LOG2E), length, window, groups, masked_ref)
+    mine = lax.broadcasted_iota(jnp.int32, (length, wide), 0)
+    other = lax.broadcasted_iota(jnp.int32, (length, wide), 1) % length
+    row_off = (mine // window // cut) != (other // window // cut)
+    col_off = (mine % window // cut) != (other % window // cut)
+    for g in range(groups):
+        bias = masked_ref[0, g]
+        masked_ref[1, g] = jnp.where(col_off, bias + MASK_FILL * LOG2E, bias)
+        masked_ref[2, g] = jnp.where(row_off, bias + MASK_FILL * LOG2E, bias)
+        masked_ref[3, g] = jnp.where(row_off | col_off, bias + MASK_FILL * LOG2E, bias)
+    small[...] = jnp.zeros_like(small)
+
+    def gather_rows(a, ref, out_ref):
+        def shifted(i):
+            if i + cut < rows:
+                row, edge = ref[i + cut], col_get[a, (i + cut) // 2]
+            else:
+                row, edge = row_get[a, i + cut - rows], diag_get[a, (i + cut - rows) // 2]
+            row, edge = row.astype(f32), edge.astype(f32)
+            turned = [half_turn(row[k * window : (k + 1) * window], 0) for k in range(across)]
+            turned.append(half_turn(edge, 0) if i % 2 == 0 else edge)
+            return [jnp.where(low_sub, turned[k], turned[k + 1]) for k in range(across)]
+
+        for i in range(0, rows, 2):
+            one, two = shifted(i), shifted(i + 1)
+            for k in range(across):
+                begin = (i // window * across + k) * length + i % window * window
+                out_ref[begin : begin + 2 * window] = jnp.concatenate([one[k], two[k]], 0).astype(b16)
+
+    def settle(a, ref, out_ref):
+        for copy in halos[3 * a : 3 * a + 3]:
+            copy.wait()
+        gather_rows(a, ref, out_ref)
+
+    settle(0, tok, flat_ref)
+    loads[2].wait()
+    loads[3].wait()
+
+    row_base, col_base = ha * rows, wa * cols
+    qkv_ref[...] = mxu(flat_ref[...], w_qkv_ref[...], NN).astype(b16)
+    lane_ones = same_block(lanes, wide, head_dim, length)
+    lane_lane = same_block(lanes, lanes, head_dim, head_dim)
+    pick = same_block(head_rows, depth, 1, head_dim)
+    high, low = split(jnp.square(qkv_ref[:, :depth].astype(f32)))
+    q_sums = mxu(pick, high, NT) + mxu(pick, low, NT)
+    q_rows = lax.rsqrt(q_sums + 1.0) * scale[:, :1]
+    half = lax.broadcasted_iota(jnp.int32, (1, 2 * length), 1) < length
+    for j in range(count // 2):
+        base = q_rows[:, j * 2 * length : (j + 1) * 2 * length]
+        turned = half_turn(base, 1)
+        for g in range(groups):
+            for p in range(GROUP // 2):
+                one, two = g * GROUP + 2 * p, g * GROUP + 2 * p + 1
+                place = slice(p * 2 * length, (p + 1) * 2 * length)
+                qrow_ref[2 * j, g, :, place] = jnp.where(half, base[one : one + 1], turned[two : two + 1])
+                qrow_ref[2 * j + 1, g, :, place] = jnp.where(half, turned[one : one + 1], base[two : two + 1])
+    for g in range(groups):
+        query = qkv_ref[:, g * lanes : (g + 1) * lanes].astype(f32)
+        key = qkv_ref[:, depth + g * lanes : depth + (g + 1) * lanes].astype(f32)
+        high, low = split(jnp.square(key))
+        kinv_ref[g] = lax.rsqrt(mxu(high, lane_ones, NN) + mxu(low, lane_ones, NN) + 1.0)
+        norm_ref[1, g] = 1.0 / (mxu(high, lane_lane, NN) + mxu(low, lane_lane, NN) + 1.0)
+        high, low = split(jnp.square(query))
+        norm_ref[0, g] = 1.0 / (mxu(high, lane_lane, NN) + mxu(low, lane_lane, NN) + 1.0)
+
+    def load(ref, w, g, part):
+        return ref[
+            pl.ds(pl.multiple_of(w * length, length), length),
+            part * depth + g * lanes : part * depth + (g + 1) * lanes,
+        ]
+
+    def forward(step, carry):
+        units = [(step * FWD + k, g) for k in range(FWD) for g in range(groups)]
+        scores = []
+        for w, g in units:
+            query, key = load(qkv_ref, w, g, 0), load(qkv_ref, w, g, 1)
+            raw = mxu(key, tile_heads(query, head_dim), NT)
+            last_row = (row_base + w // across * window) // (height - window)
+            last_col = (col_base + w % across * window) // (width - window)
+            kinv = kinv_ref[g, pl.ds(pl.multiple_of(w * length, length), length), :]
+            scores.append(raw * kinv * (qrow_ref[w, g] * LOG2E) + masked_ref[last_row * 2 + last_col, g])
+        for (w, g), score in zip(units, scores):
+            expo = jnp.exp2(score - jnp.max(score, 0, keepdims=True))
+            probs = expo * (1.0 / jnp.sum(expo, 0, keepdims=True))
+            probs_ref[w, g] = probs
+            att = gather_heads(mxu(probs.astype(b16), load(qkv_ref, w, g, 2), TN), head_dim, length)
+            att_ref[
+                pl.ds(pl.multiple_of(w * length, length), length), g * lanes : (g + 1) * lanes
+            ] = att.astype(b16)
+        return carry
+
+    lax.fori_loop(0, count // FWD, forward, 0)
+
+    settle(1, cot, grad_ref)
+    proj = mxu(att_ref[...], w_proj_ref[...], NN)
+    centre = proj - jnp.mean(proj, -1, keepdims=True)
+    inv_std = lax.rsqrt(jnp.mean(centre * centre, -1, keepdims=True) + EPS_NORM)
+    normed = centre * inv_std
+    upstream = grad_ref[...].astype(f32)
+    d_gain = jnp.sum(upstream * normed, 0, keepdims=True)
+    scaled = upstream * gain_ref[...].reshape(1, depth)
+    d_proj = inv_std * (
+        scaled
+        - jnp.mean(scaled, -1, keepdims=True)
+        - normed * jnp.mean(scaled * normed, -1, keepdims=True)
+    )
+    d_proj = d_proj.astype(b16)
+    small[heads : heads + 1, :] = d_gain[:, :span]
+    small[heads + 1 : heads + 2, : depth - span] = d_gain[:, span:]
+    per = len(chunk_refs) // 4
+    chunks = [chunk_refs[c * per : (c + 1) * per] for c in range(4)]
+    flying = {}
+
+    def begin(c):
+        core_send, core_mine, core_get = chunks[c][:3]
+        w = core_send.shape[0] // 2
+        for side_of in range(2):
+            here = slice(side_of * w, (side_of + 1) * w)
+            base = 2 * side_of * w
+            theirs = pl.ds(pl.multiple_of(base + (1 - core) * w, 32), w)
+            core_send[here] = product_ref[theirs, :].astype(b16)
+        flying[c] = start(core_send, core_get, chunks[c][9], partner)
+        for side_of in range(2):
+            here = slice(side_of * w, (side_of + 1) * w)
+            core_mine[here] = product_ref[pl.ds(pl.multiple_of(2 * side_of * w + core * w, 32), w), :]
+
+    def cross(c):
+        core_send, core_mine, core_get, plane_send, plane_get = chunks[c][:5]
+        flying[c].wait()
+        core_mine[...] = core_mine[...] + core_get[...].astype(f32)
+        w = plane_send.shape[1]
+        flying[c] = []
+        for k, (b, y, device) in enumerate(((1 - ba, wa, image), (ba, 1 - wa, side), (1 - ba, 1 - wa, corner))):
+            place = pl.ds(pl.multiple_of((2 * b + y) * w, 32), w)
+            plane_send[k] = core_mine[place, :].astype(b16)
+            flying[c].append(start(plane_send.at[k], plane_get.at[k], chunks[c][10].at[k], device))
+
+    def scatter(c):
+        core_mine, plane_get, near_send, near_get = chunks[c][1], chunks[c][4], chunks[c][5], chunks[c][6]
+        for copy in flying[c]:
+            copy.wait()
+        w = plane_get.shape[1]
+        total = core_mine[pl.ds(pl.multiple_of((2 * ba + wa) * w, 32), w), :]
+        for k in range(3):
+            total = total + plane_get[k].astype(f32)
+        r = near_send.shape[1]
+        for j in range(chips):
+            near_send[j] = total[j * r : (j + 1) * r].astype(b16)
+        flying[c] = []
+        for step in range(1, chips):
+            far_chip = lax.rem(ha // 2 + step, chips)
+            flying[c].append(
+                start(
+                    near_send.at[far_chip], near_get.at[step - 1], chunks[c][11].at[step - 1],
+                    (2 * far_chip + core, wa, ba),
+                )
+            )
+
+    def gather(c):
+        near_send, near_get, whole = chunks[c][5:8]
+        for copy in flying[c]:
+            copy.wait()
+        total = near_send[ha // 2].astype(f32)
+        for step in range(1, chips):
+            total = total + near_get[step - 1].astype(f32)
+        whole[me] = total.astype(b16)
+        flying[c] = []
+        for step in range(1, peers):
+            flying[c].append(start(whole.at[me], whole.at[me], chunks[c][12].at[step - 1], peer(step)[1]))
+
+    def mirror(c):
+        whole, core_all = chunks[c][7:9]
+        for copy in flying[c]:
+            copy.wait()
+        flying[c] = start(whole, core_all, chunks[c][13], partner)
+        put(c, whole, core)
+
+    def finish(c):
+        flying[c].wait()
+        put(c, chunks[c][8], 1 - core)
+
+    def put(c, source, which):
+        r = source.shape[1]
+        w = peers * r
+        begin_rows = half_starts[c]
+        step_rows = lanes // 2
+        for first in range(0, 2 * w, step_rows):
+            near, away = begin_rows[first // step_rows]
+            for j in range(first % w // r, min(peers, (first % w + step_rows) // r)):
+                inside = j * r - first % w
+
+                def one(is_wq, near_row, away_row, out):
+                    row = jnp.where(ba == 0, near_row, away_row) + inside
+                    out[pl.ds(pl.multiple_of(row, 8), r), :] = source[j].astype(f32)
+
+                @pl.when(which == first // w)
+                def _():
+                    one(near[0], near[1], away[1], near[0])
+
+    unit = lanes // 2
+    half_starts = [
+        [((wp_out, k * unit), (wp_out, (1 + k) * unit)) for k in range(2)],
+        [((wq_out, k * unit), (wq_out, (3 + k) * unit)) for k in range(2)],
+        [((wq_out, (4 + k) * unit), (wq_out, (1 + k if k < 2 else 5 + k) * unit)) for k in range(4)],
+        [
+            ((wq_out, 2 * unit), (wq_out, 5 * unit)), ((wq_out, 3 * unit), (wq_out, 6 * unit)),
+            ((wq_out, 8 * unit), (wq_out, 0)), ((wp_out, 2 * unit), (wp_out, 0)),
+        ],
+    ]
+
+    product = mxu(d_proj, att_ref[...], TN)
+    product_ref[:lanes] = product[:lanes]
+    p_mid[...] = product[lanes : 2 * lanes]
+    product_ref[lanes : 2 * lanes] = product[2 * lanes :]
+    begin(0)
+    d_att_ref[...] = mxu(d_proj, w_proj_ref[...], NT).astype(b16)
+
+    def backward_group(g):
+        def backward(step, total):
+            units = [step * BWD + k for k in range(BWD)]
+            grads = []
+            for w in units:
+                d_tall = tile_heads(load(d_att_ref, w, g, 0), head_dim)
+                d_probs = mxu(load(qkv_ref, w, g, 2), d_tall, NT)
+                d_value = mxu(probs_ref[w, g].astype(b16), d_tall, NN)
+                d_qkv_ref[
+                    pl.ds(pl.multiple_of(w * length, length), length),
+                    2 * depth + g * lanes : 2 * depth + (g + 1) * lanes,
+                ] = d_value.astype(b16)
+                grads.append(d_probs)
+            summed = d_bias_ref[g]
+            for w, d_probs in zip(units, grads):
+                place = pl.ds(pl.multiple_of(w * length, length), length)
+                probs = probs_ref[w, g]
+                d_scores = probs * (d_probs - jnp.sum(d_probs * probs, 0, keepdims=True))
+                summed = summed + d_scores
+                high, low = split(d_scores * kinv_ref[g, place, :] * qrow_ref[w, g])
+                both = jnp.concatenate([high, low], 0)
+                query, key = load(qkv_ref, w, g, 0), load(qkv_ref, w, g, 1)
+                pair = mxu(both, tile_heads(query, head_dim), NN)
+                raw_k_ref[place, :] = pair[:length] + pair[length:]
+                tall = mxu(both, jnp.concatenate([key, key], 0), TN)
+                raw_q_ref[place, :] = gather_heads(tall, head_dim, length)
+            d_bias_ref[g] = summed
+            return total
+
+        d_bias_ref[g] = jnp.zeros((length, wide), f32)
+        lax.fori_loop(0, count // BWD, backward, 0)
+        for part, ref in enumerate((raw_q_ref, raw_k_ref)):
+            place = slice(part * depth + g * lanes, part * depth + (g + 1) * lanes)
+            value, grad = qkv_ref[:, place].astype(f32), ref[...]
+            along = value * grad
+            if part == 0:
+                spot = depth - span + g * lanes
+                small[
+                    heads + 1 + spot // span : heads + 2 + spot // span, spot % span : spot % span + lanes
+                ] = jnp.sum(along, 0, keepdims=True)
+            d_qkv_ref[:, place] = (
+                grad - value * norm_ref[part, g] * mxu_fine(along, lane_lane, NN)
+            ).astype(b16)
+
+    def dense_column(row, part, g, rows_from=0, rows_to=None):
+        place = slice(part * depth + g * lanes, part * depth + (g + 1) * lanes)
+        product_ref[row : row + lanes] = mxu(d_qkv_ref[:, place], flat_ref[...], TN)
+
+    backward_group(0)
+    dense_column(0, 0, 0)
+    dense_column(lanes, 2, 0)
+    begin(1)
+    cross(0)
+    backward_group(2)
+    dense_column(0, 0, 2)
+    dense_column(lanes, 1, 0)
+    dense_column(2 * lanes, 1, 2)
+    dense_column(3 * lanes, 2, 2)
+    begin(2)
+    cross(1)
+    backward_group(1)
+    dense_column(0, 0, 1)
+    dense_column(2 * lanes, 2, 1)
+    key = mxu(d_qkv_ref[:, depth + lanes : depth + 2 * lanes], flat_ref[...], TN)
+    product_ref[lanes : lanes + unit] = key[:unit]
+    product_ref[lanes + unit : 2 * lanes] = p_mid[:unit]
+    product_ref[3 * lanes : 3 * lanes + unit] = key[unit:]
+    product_ref[3 * lanes + unit : 4 * lanes] = p_mid[unit:]
+    begin(3)
+    scatter(0)
+    cross(2)
+    d_flat_ref[...] = mxu(d_qkv_ref[...], w_qkv_ref[...], NT).astype(b16)
+
+    def back_tiles(i):
+        begin_row = i // window * across * length + i % window * window
+        return [
+            half_turn(d_flat_ref[begin_row + k * length : begin_row + k * length + window].astype(f32), 0)
+            for k in range(across)
+        ]
+
+    for i in range(0, rows, 2):
+        one, two = back_tiles(i), back_tiles(i + 1)
+        col_back[i // 2] = jnp.where(low_sub, one[-1], half_turn(two[-1], 0)).astype(b16)
+        if i >= rows - cut:
+            row_back[i - (rows - cut)] = jnp.concatenate(one, 0).astype(b16)
+            row_back[i + 1 - (rows - cut)] = jnp.concatenate(two, 0).astype(b16)
+    far = (rows - cut) // 2
+    back = [
+        start(row_back, row_back_get, back_sems.at[0], (below, wa, ba)),
+        start(col_back.at[pl.ds(0, far)], col_back_get, back_sems.at[1], (ha, right, ba)),
+        start(col_back.at[pl.ds(far, cut // 2)], diag_back_get, back_sems.at[2], (below, right, ba)),
+    ]
+    cross(3)
+    for k, row in enumerate(fold_bias([d_bias_ref[g] for g in range(groups)], length, window, span)):
+        small[k : k + 1, :] = row
+    tiny = start(small, small_core, tiny_sems.at[0], partner)
+    scatter(1)
+    gather(0)
     tiny.wait()
-    small_a[...] = small_ref[...] + small_core[...]
+    small_a[...] = small[...] + small_core[...]
     tiny = start(small_a, small_image, tiny_sems.at[1], image)
-    big.wait()
-
-    def halves(first):
-        q = wqkv_ref[mine, first * q_half : (first + 1) * q_half]
-        p = wproj_ref[mine, first * p_half : (first + 1) * p_half]
-        gq = core_get[:, first * q_half : (first + 1) * q_half]
-        gp = core_get[:, 2 * q_half + first * p_half : 2 * q_half + (first + 1) * p_half]
-        return q + gq.astype(f32), p + gp.astype(f32)
-
-    low, high = halves(0), halves(1)
-    for part, (a, b) in enumerate(zip(low, high)):
-        place = slice(0, q_half) if part == 0 else slice(q_half, q_half + p_half)
-        image_send[:, place] = jnp.where(ba == 0, b, a).astype(b16)
-        image_keep[:, place] = jnp.where(ba == 0, a, b)
-    big = start(image_send, image_get, image_sems, image)
+    scatter(2)
     tiny.wait()
     small_b[...] = small_a[...] + small_image[...]
     tinies = []
     for step in range(1, peers):
         tinies.append(start(small_b, small_near.at[step - 1], tiny_sems.at[step + 1], peer(step)[1]))
-    big.wait()
-    total = image_keep[...] + image_get[...].astype(f32)
-    r, c = near_send.shape[1:]
-    split_c = total.shape[1] // c
-    for j in range(peers):
-        row, col = j // split_c * r, j % split_c * c
-        near_send[j] = total[row : row + r, col : col + c].astype(b16)
-    copies = []
-    for step in range(1, peers):
-        other, device = peer(step)
-        copies.append(start(near_send.at[other], near_get.at[step - 1], near_sems.at[step - 1], device))
+
+    def put_row(i, turned, edge, odd):
+        ahead = [half_turn(edge, 0) if odd else edge] + turned
+        out = [jnp.where(low_sub, ahead[k], ahead[k + 1]) for k in range(across)]
+        d_tok_ref[i] = (jnp.concatenate(out, 0) + cot[i].astype(f32)).astype(b16)
+
+    back[1].wait()
+    for i in range(rows - cut):
+        put_row(i + cut, back_tiles(i), col_back_get[i // 2].astype(f32), i % 2 == 1)
+    gather(1)
+    scatter(3)
+    back[0].wait()
+    back[2].wait()
+    for i in range(cut):
+        whole_row = row_back_get[i].astype(f32)
+        turned = [whole_row[k * window : (k + 1) * window] for k in range(across)]
+        put_row(i, turned, diag_back_get[i // 2].astype(f32), i % 2 == 1)
+    gather(2)
+    mirror(0)
+    mirror(1)
+    gather(3)
     for copy in tinies:
         copy.wait()
-    small = small_b[...]
+    total = small_b[...]
     for step in range(1, peers):
-        small = small + small_near[step - 1]
-    small_out[...] = small
+        total = total + small_near[step - 1]
+    table_out[...] = (total[: head_rows] * (BIAS_RANGE * sigma * (1.0 - sigma)))[:heads, :entries]
+    gain_row = jnp.concatenate([total[heads : heads + 1, :], total[heads + 1 : heads + 2, : depth - span]], 1)
+    gain_out[...] = gain_row.reshape(depth)
+    sums = jnp.concatenate([total[heads + 1 : heads + 2, depth - span :], total[heads + 2 : heads + 3, :]], 1)
+    sums = mxu_fine(jnp.broadcast_to(sums, (8, depth)), same_block(depth, 128, head_dim, 1), NN)[:1]
+    at = lax.broadcasted_iota(jnp.int32, (1, 128), 1)
+    logits = jnp.zeros((1, 128), f32)
+    for h in range(heads):
+        logits = jnp.where(at == h, scale_ref[h], logits)
+    scale_out[...] = jnp.where(logits < SCALE_CAP, sums, 0.0).reshape(128)[:heads]
+    finish(0)
+    finish(1)
+    mirror(2)
+    finish(2)
+    mirror(3)
+    finish(3)
+
+
+def finish_kernel(*refs):
+    count = len(refs) // 2
+    sems = refs[-1]
+    copies = [pltpu.make_async_copy(refs[k], refs[count + k], sems.at[k]) for k in range(count)]
+    for copy in copies:
+        copy.start()
     for copy in copies:
         copy.wait()
-    total = near_send[me].astype(f32)
-    for step in range(1, peers):
-        total = total + near_get[step - 1].astype(f32)
-    own[...] = total.astype(b16)
-    whole[me] = own[...]
-    copies = []
-    for step in range(1, peers):
-        _, device = peer(step)
-        copies.append(start(own, whole.at[me], all_sems.at[step - 1], device))
-    for copy in copies:
-        copy.wait()
-    last = start(whole, core_all, last_sems, partner)
-
-    def put(source, first):
-        for j in range(peers):
-            row, col = j // split_c * r, j % split_c * c
-            block = source[j].astype(f32)
-            rows = pl.ds(pl.multiple_of(first * half + row, 8), r)
-            q_part = max(0, min(c, q_half - col))
-            if q_part > 0:
-                qkv_out[rows, col : col + q_part] = block[:, :q_part]
-            if q_part < c:
-                begin = col + q_part - q_half
-                proj_out[rows, begin : begin + c - q_part] = block[:, q_part:]
-
-    put(whole, core)
-    last.wait()
-    put(core_all, 1 - core)
-
-
-def reduce_all(d_wqkv, d_wproj, small):
+
+
+def whole_grads(tokens, cotangent, w_qkv, w_proj, table_logits, logit_scale, gain, height, width, window):
     size_h, size_w = lax.axis_size("ha"), lax.axis_size("wa")
     peers = size_h // 2 * size_w
-    depth = d_wqkv.shape[0]
+    f32, b16 = jnp.float32, jnp.bfloat16
+    images, rows, cols, depth = tokens.shape
+    heads = logit_scale.shape[0]
+    entries = table_logits.shape[1]
+    groups = heads // GROUP
+    lanes = depth // groups
+    length = window * window
+    wide = GROUP * length
+    total = rows * cols
+    count = total // length
+    cut = window // 2
+    span = 256
+    head_rows = -(-heads // 16) * 16
     half = depth // 2
-    cols = (d_wqkv.shape[1] + d_wproj.shape[1]) // 2
-    split_c = 2
-    r, c = half * split_c // peers, cols // split_c
-    f32, b16 = jnp.float32, jnp.bfloat16
-    tiny = small.shape
-    return pl.pallas_call(
-        functools.partial(reduce_kernel, (size_h, size_w)),
+    chips = size_h // 2
+    dma, vmem = pltpu.SemaphoreType.DMA, pltpu.VMEM
+    chunk_scratch = []
+    for w in (lanes // 2, lanes // 2, lanes, lanes):
+        r = w // peers
+        chunk_scratch += [
+            vmem((2 * w, depth), b16), vmem((2 * w, depth), f32), vmem((2 * w, depth), b16),
+            vmem((3, w // 2, depth), b16), vmem((3, w // 2, depth), b16),
+            vmem((chips, r, depth), b16), vmem((chips - 1, r, depth), b16),
+            vmem((peers, r, depth), b16), vmem((peers, r, depth), b16),
+            dma((2,)), dma((3, 2)), dma((chips - 1, 2)), dma((peers - 1, 2)), dma((2,)),
+        ]
+    small = (16, span)
+    anywhere = pl.BlockSpec(memory_space=pltpu.HBM)
+    pinned = [
+        pltpu.with_memory_space_constraint(x, pltpu.HBM)
+        for x in (tokens, cotangent, w_qkv, w_proj, table_logits, gain)
+    ]
+    outs = pl.pallas_call(
+        functools.partial(whole_kernel, (size_h, size_w), height, width, window),
         out_shape=[
-            jax.ShapeDtypeStruct((depth, d_wqkv.shape[1] // 2), f32),
-            jax.ShapeDtypeStruct((depth, d_wproj.shape[1] // 2), f32),
-            jax.ShapeDtypeStruct(tiny, f32),
+            jax.ShapeDtypeStruct((rows, cols, depth), b16),
+            jax.ShapeDtypeStruct((3 * depth // 2, depth), f32),
+            jax.ShapeDtypeStruct((depth // 2, depth), f32),
+            jax.ShapeDtypeStruct((heads, entries), f32),
+            jax.ShapeDtypeStruct((heads,), f32),
+            jax.ShapeDtypeStruct((depth,), f32),
         ],
-        in_specs=[VMEM] * 3,
-        out_specs=[VMEM] * 3,
+        in_specs=[anywhere] * 6 + [pl.BlockSpec(memory_space=pltpu.SMEM)],
+        out_specs=[VMEM] * 6,
         scratch_shapes=[
-            pltpu.VMEM((half, 2 * cols), b16),
-            pltpu.VMEM((half, 2 * cols), b16),
-            pltpu.VMEM((half, cols), f32),
-            pltpu.VMEM((half, cols), b16),
-            pltpu.VMEM((half, cols), b16),
-            pltpu.VMEM((peers, r, c), b16),
-            pltpu.VMEM((peers - 1, r, c), b16),
-            pltpu.VMEM((r, c), b16),
-            pltpu.VMEM((peers, r, c), b16),
-            pltpu.VMEM((peers, r, c), b16),
-            pltpu.VMEM(tiny, f32),
-            pltpu.VMEM(tiny, f32),
-            pltpu.VMEM(tiny, f32),
-            pltpu.VMEM(tiny, f32),
-            pltpu.VMEM((peers - 1, *tiny), f32),
-            pltpu.SemaphoreType.DMA((2,)),
-            pltpu.SemaphoreType.DMA((2,)),
-            pltpu.SemaphoreType.DMA((peers - 1, 2)),
-            pltpu.SemaphoreType.DMA((peers - 1, 2)),
-            pltpu.SemaphoreType.DMA((2,)),
-            pltpu.SemaphoreType.DMA((peers + 1, 2)),
+            vmem((rows, cols, depth), b16), vmem((rows, cols, depth), b16),
+            vmem((depth, 3 * depth), b16), vmem((depth, depth), b16),
+            vmem((heads, entries), f32), vmem((depth,), f32), vmem((head_rows, span), f32), dma((6,)),
+            vmem((2, rows // 2, window, depth), b16), vmem((2, cut, cols, depth), b16),
+            vmem((2, rows // 2, window, depth), b16), vmem((2, cut // 2, window, depth), b16), dma((2, 3, 2)),
+            vmem((total, depth), b16), vmem((total, depth), b16), vmem((total, depth), b16),
+            vmem((total, 3 * depth), b16), vmem((total, depth), b16), vmem((total, depth), b16),
+            vmem((total, 3 * depth), b16), vmem((count, groups, length, wide), f32), vmem((groups, total, wide), f32),
+            vmem((count, groups, 1, wide), f32), vmem((4, groups, length, wide), f32),
+            vmem((total, lanes), f32), vmem((total, lanes), f32), vmem((2, groups, total, lanes), f32),
+            vmem((groups, length, wide), f32), vmem((lanes, depth), f32), vmem((4 * lanes, depth), f32),
+            vmem((cut, cols, depth), b16), vmem((rows // 2, window, depth), b16), vmem((cut, cols, depth), b16),
+            vmem(((rows - cut) // 2, window, depth), b16), vmem((cut // 2, window, depth), b16), dma((3, 2)),
+            vmem(small, f32), vmem(small, f32), vmem(small, f32), vmem(small, f32), vmem(small, f32),
+            vmem((peers - 1, *small), f32), dma((peers + 1, 2)),
+            *chunk_scratch,
         ],
         compiler_params=pltpu.CompilerParams(
-            collective_id=0, has_side_effects=True, vmem_limit_bytes=48 * 2**20
+            collective_id=0, has_side_effects=True, vmem_limit_bytes=VMEM_LIMIT
         ),
-        name="reduce_all",
-    )(d_wqkv, d_wproj, small)
-
-
-def can_reduce(d_wqkv):
-    peers = lax.axis_size("ha") // 2 * lax.axis_size("wa")
-    pairs = lax.axis_size("ha") % 2 == 0 and lax.axis_size("ba") == 2
-    return pairs and peers > 1 and d_wqkv.shape[0] % peers == 0 and d_wqkv.shape[0] // peers % 16 == 0
-
-
-def pack_small(d_table, d_scale, d_gain):
-    heads, entries = d_table.shape
-    lanes = -(-entries // 128) * 128
-    flat = jnp.concatenate([d_scale, d_gain])
-    rows = -(-flat.shape[0] // lanes)
-    flat = jnp.pad(flat, (0, rows * lanes - flat.shape[0])).reshape(rows, lanes)
-    table = jnp.pad(d_table, ((0, 0), (0, lanes - entries)))
-    full = jnp.concatenate([table, flat], 0)
-    return jnp.pad(full, ((0, -full.shape[0] % 8), (0, 0)))
-
-
-def unpack_small(full, heads, entries, depth):
-    flat = full[heads:].reshape(-1)
-    return full[:heads, :entries], flat[:heads], flat[heads : heads + depth]
+        name="whole_grads",
+    )(*pinned, logit_scale)
+    d_tok, half_qkv, half_proj, d_table, d_scale, d_gain = pl.pallas_call(
+        finish_kernel,
+        out_shape=[jax.ShapeDtypeStruct(x.shape, x.dtype) for x in outs],
+        in_specs=[VMEM] * 6,
+        out_specs=[anywhere] * 6,
+        scratch_shapes=[dma((6,))],
+        compiler_params=pltpu.CompilerParams(vmem_limit_bytes=FINISH_LIMIT),
+        name="finish",
+    )(*outs)
+    return d_tok[None], half_qkv.T, half_proj.T, d_table, d_scale, d_gain
+
+
+def can_join(tokens, logit_scale):
+    size_h, size_w, size_b = (lax.axis_size(name) for name in ("ha", "wa", "ba"))
+    images, rows, cols, depth = tokens.shape
+    peers = size_h // 2 * size_w
+    return (
+        images == 1 and size_b == 2 and size_w == 2 and size_h % 2 == 0 and size_h > 2
+        and logit_scale.shape[0] == 3 * GROUP and depth == 3 * 128 and WIN == 8
+        and rows % WIN == 0 and cols % (2 * WIN) == 0 and rows * cols // 64 % BWD == 0
+        and 64 % peers == 0 and 64 // peers % 8 == 0
+    )
 
 
 def shift_in(tokens, cotangent, shift):
@@ -529,27 +990,22 @@
     width = cols * lax.axis_size("wa")
     row_base = lax.axis_index("ha") * rows
     col_base = lax.axis_index("wa") * cols
+    if can_join(tokens, logit_scale):
+        return whole_grads(
+            tokens, cotangent, w_qkv, w_proj, table_logits, logit_scale, gain, height, width, WIN
+        )
     params = (w_qkv, w_proj, table_logits, logit_scale, gain)
     moved, moved_grad = shift_in(tokens, cotangent, shift)
     d_moved, parts = local_grads(moved, moved_grad, row_base, col_base, height, width, WIN, params)
     back = shift_out(d_moved, shift)
     d_tokens = (cotangent.astype(jnp.float32) + back.astype(jnp.float32)).astype(jnp.bfloat16)
     d_wqkv, d_wproj, d_table, d_scale, d_gain = parts
-    if can_reduce(d_wqkv):
-        small = pack_small(d_table, d_scale, d_gain)
-        half_qkv, half_proj, small = reduce_all(d_wqkv, d_wproj, small)
-        d_table, d_scale, d_gain = unpack_small(small, *d_table.shape, d_gain.shape[0])
-    else:
-        half_qkv, half_proj = (
-            lax.psum_scatter(d_wqkv.astype(jnp.bfloat16), "ba", scatter_dimension=1, tiled=True).astype(
-                jnp.float32
-            ),
-            lax.psum_scatter(
-                d_wproj.astype(jnp.bfloat16), "ba", scatter_dimension=1, tiled=True
-            ).astype(jnp.float32),
-        )
-        half_qkv, half_proj = lax.psum((half_qkv, half_proj), ("ha", "wa"))
-        d_table, d_scale, d_gain = lax.psum((d_table, d_scale, d_gain), ("ha", "wa", "ba"))
+    half_qkv, half_proj = (
+        lax.psum_scatter(d_wqkv.astype(jnp.bfloat16), "ba", scatter_dimension=1, tiled=True).astype(jnp.float32),
+        lax.psum_scatter(d_wproj.astype(jnp.bfloat16), "ba", scatter_dimension=1, tiled=True).astype(jnp.float32),
+    )
+    half_qkv, half_proj = lax.psum((half_qkv, half_proj), ("ha", "wa"))
+    d_table, d_scale, d_gain = lax.psum((d_table, d_scale, d_gain), ("ha", "wa", "ba"))
     return (d_tokens, half_qkv, half_proj, d_table, d_scale, d_gain)
 
 

time: 70.7 us -> 46.3 us (0.65)
  starting transfers between devices: 8.1 us -> 0 us
  local copies, waits for them, and re-layouts: 6.93 us -> 0.65 us
  other arithmetic: 5.88 us -> 0 us
  waiting for transfers between devices: 5.02 us -> 0 us
  Pallas kernels: 40.3 us -> 44.8 us
  matrix products: 2.98 us -> 0 us
    ppermute x4 -> x0, starting transfers between devices: 8.1 us -> none  [from_behind(): return lax.ppermute(block, axis, route)]
    ppermute x4 -> x0, waiting for transfers between devices: 5.02 us -> none  [from_behind(): return lax.ppermute(block, axis, route)]
    pallas_call x2, Pallas kernels: 40.3 us -> 44.8 us  [the longest x1 43.6 us: whole_grads(): pl.pallas_call(functools.partial(whole_kernel, (size_h, size_w), height,...]
    unnamed x29 -> x2, local copies, waits for them, and re-layouts: 4.15 us -> 0.65 us
    dot_general x2 -> x0, matrix products: 2.98 us -> none  [the longest x1 1.52 us: local_grads(): lax.dot_general(three_parts(heads_bias), hot, NT, preferred_element_type=...]
    another operation x4 -> x0, other arithmetic: 1.83 us -> none  [the longest x2 1.05 us: shift_in(): stacked = jnp.stack([tokens, cotangent])]
    slice x3 -> x0, local copies, waits for them, and re-layouts: 1.81 us -> none  [the longest x2 1.16 us: unpack_small(): return (full[:heads, :entries], flat[:heads], flat[heads:heads + depth])]
    convert_element_type x1 -> x0, other arithmetic: 1.68 us -> none  [shards(): (cotangent.astype(jnp.float32) + back.astype(jnp.float32)).astype(jnp.bfl...]
  transfers between devices with their start and end apart: 4 -> 0, of which waited for: 2 -> 0; matrix products, arithmetic and copies ran while one was open for 13% -> 0% of each run, Pallas kernels for 42% -> 0%
where the time goes in v2:
time: 46.3 us; the launch traced here: 46.1 us
  Pallas kernels  44.8 us (97%)
  local copies, waits for them, and re-layouts  0.65 us (1%)
  between operations  0.65 us (1%)
    pallas_call x1, Pallas kernels, whole_grads(): pl.pallas_call(functools.partial(whole_kernel, (size_h, size_w), height,...  43.6 us
    pallas_call x1, Pallas kernels, whole_grads(): pl.pallas_call(finish_kernel, out_shape=[jax.ShapeDtypeStruct(x.shape, x....  1.2 us

profile of v2, /device:TPU:0, one launch (start us, length us, event | category | flops | bytes accessed | tf_op | source)
XLA Modules:
  0.0 46.1 jit_solution(2421461866605885998)
XLA Ops:
  0.6 0.0 copy-start
  0.6 0.6 %copy-done = f32[12]{0:T(128)S(1)} copy-done((f32[12]{0:T(128)S(1)}, f32[12]{0:T(128)}, u32[]{:S(2)}) %copy-start) | copy-done | bytes 72
  1.3 43.6 %whole_grads.1 = (bf16[16,32,384]{2,1,0:T(8,128)(2,1)S(1)}, f32[576,384]{1,0:T(8,128)S(1)}, f32[192,384]{1,0:T(8,128)S(1)}, f32[12,225]{1,0:T(8,128)S(1)}, f32[12]{0:T(128)S(1)}, /*index=5*/f32[384]{0:T(512)S(1)}) custom-call(bf16[1,16,32,384]{3,2,1,0:T(8,128)(2,1)} %tokens_ref.1, bf16[1,16,32,384]{3,2,1,0:T(8,128)(2,1)} %cot_ref.1, ...), custom_call_target="tpu_custom_call" | custom-call | tf_op jit(solution)/shard_map/whole_grads/pallas_call | solution.py:908
  44.9 1.2 %finish.1 = (bf16[16,32,384]{2,1,0:T(8,128)(2,1)}, f32[576,384]{1,0:T(8,128)}, f32[192,384]{1,0:T(8,128)}, f32[12,225]{1,0:T(8,128)}, f32[12]{0:T(128)}, /*index=5*/f32[384]{0:T(512)}) custom-call(bf16[16,32,384]{2,1,0:T(8,128)(2,1)S(1)} %get-tuple-element.18.refs_0_, f32[576,384]{1,0:T(8,128)S(1)} %get-tuple-element.19.refs_1_, ...), custom_call_target="tpu_custom_call" | custom-call | tf_op jit(solution)/shard_map/finish/pallas_call | solution.py:943
Async XLA Ops:
  0.6 0.7 %copy-start = (f32[12]{0:T(128)S(1)}, f32[12]{0:T(128)}, u32[]{:S(2)}) copy-start(f32[12]{0:T(128)} %scale_ref.1) | copy-start | bytes 148

commit v3 on v2

--- a/solution.py
+++ b/solution.py
@@ -400,14 +400,14 @@
 def whole_kernel(
     shape, height, width, window,
     tokens_ref, cot_ref, w_qkv_hbm, w_proj_hbm, table_hbm, gain_hbm, scale_ref,
-    d_tok_ref, wq_out, wp_out, table_out, scale_out, gain_out,
+    d_tok_ref, grads_out, table_out, scale_out, gain_out,
     tok, cot, w_qkv_ref, w_proj_ref, table_in, gain_ref, table_ref, local_sems,
     col_send, row_get, col_get, diag_get, halo_sems,
-    flat_ref, grad_ref, d_flat_ref,
+    flat_ref, grad_ref, d_flat_ref, d_proj_ref,
     qkv_ref, att_ref, d_att_ref, d_qkv_ref, probs_ref, kinv_ref, qrow_ref, masked_ref, raw_q_ref, raw_k_ref,
-    norm_ref, d_bias_ref, p_mid, product_ref,
+    norm_ref, d_bias_ref, p_mid, k_first, product_ref,
     row_back, col_back, row_back_get, col_back_get, diag_back_get, back_sems,
-    small, small_core, small_a, small_image, small_b, small_near, tiny_sems,
+    small, small_core, small_a, small_image, small_b, small_side, small_c, small_near, small_total, tiny_sems,
     *chunk_refs,
 ):
     size_h, size_w = shape
@@ -464,20 +464,27 @@
     wide = GROUP * length
     low_sub = lax.broadcasted_iota(jnp.int32, (window, depth), 0) < cut
 
-    for a, ref in enumerate((tok, cot)):
+    def pack_columns(a, ref):
         loads[a].wait()
         for j in range(rows // 2):
             first = ref[2 * j, :window, :].astype(f32)
             second = ref[2 * j + 1, :window, :].astype(f32)
             col_send[a, j] = jnp.where(low_sub, first, half_turn(second, 0)).astype(b16)
+
+    halos = {}
+
+    def send_halo(a, ref):
+        halos[a, 0] = start(col_send.at[a], col_get.at[a], halo_sems.at[a, 1], (ha, left, ba))
+        halos[a, 1] = start(ref.at[pl.ds(0, cut)], row_get.at[a], halo_sems.at[a, 0], (above, wa, ba))
+        halos[a, 2] = start(
+            col_send.at[a, pl.ds(0, cut // 2)], diag_get.at[a], halo_sems.at[a, 2], (above, left, ba)
+        )
+
+    pack_columns(0, tok)
     pl.semaphore_wait(barrier, len(targets))
-    halos = []
-    for a, ref in enumerate((tok, cot)):
-        halos.append(start(ref.at[pl.ds(0, cut)], row_get.at[a], halo_sems.at[a, 0], (above, wa, ba)))
-        halos.append(start(col_send.at[a], col_get.at[a], halo_sems.at[a, 1], (ha, left, ba)))
-        halos.append(
-            start(col_send.at[a, pl.ds(0, cut // 2)], diag_get.at[a], halo_sems.at[a, 2], (above, left, ba))
-        )
+    send_halo(0, tok)
+    pack_columns(1, cot)
+    send_halo(1, cot)
 
     loads[4].wait()
     loads[5].wait()
@@ -504,7 +511,7 @@
         masked_ref[3, g] = jnp.where(row_off | col_off, bias + MASK_FILL * LOG2E, bias)
     small[...] = jnp.zeros_like(small)
 
-    def gather_rows(a, ref, out_ref):
+    def gather_rows(a, ref, out_ref, from_row, to_row):
         def shifted(i):
             if i + cut < rows:
                 row, edge = ref[i + cut], col_get[a, (i + cut) // 2]
@@ -515,47 +522,48 @@
             turned.append(half_turn(edge, 0) if i % 2 == 0 else edge)
             return [jnp.where(low_sub, turned[k], turned[k + 1]) for k in range(across)]
 
-        for i in range(0, rows, 2):
+        for i in range(from_row, to_row, 2):
             one, two = shifted(i), shifted(i + 1)
             for k in range(across):
                 begin = (i // window * across + k) * length + i % window * window
                 out_ref[begin : begin + 2 * window] = jnp.concatenate([one[k], two[k]], 0).astype(b16)
 
-    def settle(a, ref, out_ref):
-        for copy in halos[3 * a : 3 * a + 3]:
-            copy.wait()
-        gather_rows(a, ref, out_ref)
-
-    settle(0, tok, flat_ref)
-    loads[2].wait()
-    loads[3].wait()
-
     row_base, col_base = ha * rows, wa * cols
-    qkv_ref[...] = mxu(flat_ref[...], w_qkv_ref[...], NN).astype(b16)
     lane_ones = same_block(lanes, wide, head_dim, length)
     lane_lane = same_block(lanes, lanes, head_dim, head_dim)
     pick = same_block(head_rows, depth, 1, head_dim)
-    high, low = split(jnp.square(qkv_ref[:, :depth].astype(f32)))
-    q_sums = mxu(pick, high, NT) + mxu(pick, low, NT)
-    q_rows = lax.rsqrt(q_sums + 1.0) * scale[:, :1]
     half = lax.broadcasted_iota(jnp.int32, (1, 2 * length), 1) < length
-    for j in range(count // 2):
-        base = q_rows[:, j * 2 * length : (j + 1) * 2 * length]
-        turned = half_turn(base, 1)
+
+    def project(begin_window, end_window):
+        part_rows = slice(begin_window * length, end_window * length)
+        qkv_ref[part_rows] = mxu(flat_ref[part_rows], w_qkv_ref[...], NN).astype(b16)
+        high, low = split(jnp.square(qkv_ref[part_rows, :depth].astype(f32)))
+        q_sums = mxu(pick, high, NT) + mxu(pick, low, NT)
+        q_rows = lax.rsqrt(q_sums + 1.0) * scale[:, :1]
+        for j in range(begin_window // 2, end_window // 2):
+            shifted_j = 2 * j - begin_window
+            base = q_rows[:, shifted_j * length : (shifted_j + 2) * length]
+            turned = half_turn(base, 1)
+            for g in range(groups):
+                for p in range(GROUP // 2):
+                    one, two = g * GROUP + 2 * p, g * GROUP + 2 * p + 1
+                    place = slice(p * 2 * length, (p + 1) * 2 * length)
+                    qrow_ref[2 * j, g, :, place] = jnp.where(half, base[one : one + 1], turned[two : two + 1])
+                    qrow_ref[2 * j + 1, g, :, place] = jnp.where(half, turned[one : one + 1], base[two : two + 1])
         for g in range(groups):
-            for p in range(GROUP // 2):
-                one, two = g * GROUP + 2 * p, g * GROUP + 2 * p + 1
-                place = slice(p * 2 * length, (p + 1) * 2 * length)
-                qrow_ref[2 * j, g, :, place] = jnp.where(half, base[one : one + 1], turned[two : two + 1])
-                qrow_ref[2 * j + 1, g, :, place] = jnp.where(half, turned[one : one + 1], base[two : two + 1])
-    for g in range(groups):
-        query = qkv_ref[:, g * lanes : (g + 1) * lanes].astype(f32)
-        key = qkv_ref[:, depth + g * lanes : depth + (g + 1) * lanes].astype(f32)
-        high, low = split(jnp.square(key))
-        kinv_ref[g] = lax.rsqrt(mxu(high, lane_ones, NN) + mxu(low, lane_ones, NN) + 1.0)
-        norm_ref[1, g] = 1.0 / (mxu(high, lane_lane, NN) + mxu(low, lane_lane, NN) + 1.0)
-        high, low = split(jnp.square(query))
-        norm_ref[0, g] = 1.0 / (mxu(high, lane_lane, NN) + mxu(low, lane_lane, NN) + 1.0)
+            key = qkv_ref[part_rows, depth + g * lanes : depth + (g + 1) * lanes].astype(f32)
+            high, low = split(jnp.square(key))
+            kinv_ref[g, part_rows] = lax.rsqrt(mxu(high, lane_ones, NN) + mxu(low, lane_ones, NN) + 1.0)
+
+    def norms(begin_window, end_window):
+        part_rows = slice(begin_window * length, end_window * length)
+        for g in range(groups):
+            for part in range(2):
+                place = slice(part * depth + g * lanes, part * depth + (g + 1) * lanes)
+                high, low = split(jnp.square(qkv_ref[part_rows, place].astype(f32)))
+                norm_ref[part, g, part_rows] = 1.0 / (
+                    mxu(high, lane_lane, NN) + mxu(low, lane_lane, NN) + 1.0
+                )
 
     def load(ref, w, g, part):
         return ref[
@@ -583,22 +591,45 @@
             ] = att.astype(b16)
         return carry
 
-    lax.fori_loop(0, count // FWD, forward, 0)
-
-    settle(1, cot, grad_ref)
-    proj = mxu(att_ref[...], w_proj_ref[...], NN)
-    centre = proj - jnp.mean(proj, -1, keepdims=True)
-    inv_std = lax.rsqrt(jnp.mean(centre * centre, -1, keepdims=True) + EPS_NORM)
-    normed = centre * inv_std
-    upstream = grad_ref[...].astype(f32)
-    d_gain = jnp.sum(upstream * normed, 0, keepdims=True)
-    scaled = upstream * gain_ref[...].reshape(1, depth)
-    d_proj = inv_std * (
-        scaled
-        - jnp.mean(scaled, -1, keepdims=True)
-        - normed * jnp.mean(scaled * normed, -1, keepdims=True)
-    )
-    d_proj = d_proj.astype(b16)
+    def norm_gradient(begin_window, end_window):
+        part_rows = slice(begin_window * length, end_window * length)
+        proj = mxu(att_ref[part_rows], w_proj_ref[...], NN)
+        centre = proj - jnp.mean(proj, -1, keepdims=True)
+        inv_std = lax.rsqrt(jnp.mean(centre * centre, -1, keepdims=True) + EPS_NORM)
+        normed = centre * inv_std
+        upstream = grad_ref[part_rows].astype(f32)
+        d_gain = jnp.sum(upstream * normed, 0, keepdims=True)
+        scaled = upstream * gain_ref[...].reshape(1, depth)
+        d_proj = inv_std * (
+            scaled
+            - jnp.mean(scaled, -1, keepdims=True)
+            - normed * jnp.mean(scaled * normed, -1, keepdims=True)
+        )
+        d_proj = d_proj.astype(b16)
+        d_proj_ref[part_rows] = d_proj
+        d_att_ref[part_rows] = mxu(d_proj, w_proj_ref[...], NT).astype(b16)
+        return d_gain
+
+    early = count - across
+    halos[0, 0].wait()
+    gather_rows(0, tok, flat_ref, 0, rows - window)
+    loads[2].wait()
+    project(0, early)
+    lax.fori_loop(0, early // FWD, forward, 0)
+    norms(0, early)
+    halos[1, 0].wait()
+    gather_rows(1, cot, grad_ref, 0, rows - window)
+    loads[3].wait()
+    d_gain = norm_gradient(0, early)
+    halos[0, 1].wait()
+    halos[0, 2].wait()
+    gather_rows(0, tok, flat_ref, rows - window, rows)
+    project(early, count)
+    lax.fori_loop(early // FWD, count // FWD, forward, 0)
+    halos[1, 1].wait()
+    halos[1, 2].wait()
+    gather_rows(1, cot, grad_ref, rows - window, rows)
+    d_gain = d_gain + norm_gradient(early, count)
     small[heads : heads + 1, :] = d_gain[:, :span]
     small[heads + 1 : heads + 2, : depth - span] = d_gain[:, span:]
     per = len(chunk_refs) // 4
@@ -662,54 +693,67 @@
         for step in range(1, peers):
             flying[c].append(start(whole.at[me], whole.at[me], chunks[c][12].at[step - 1], peer(step)[1]))
 
+    def spread_column(c):
+        near_send, near_get, whole = chunks[c][5:8]
+        for copy in flying[c]:
+            copy.wait()
+        total = near_send[ha // 2].astype(f32)
+        for step in range(1, chips):
+            total = total + near_get[step - 1].astype(f32)
+        whole[me] = total.astype(b16)
+        flying[c] = []
+        for step in range(1, chips):
+            far_chip = lax.rem(ha // 2 + step, chips)
+            flying[c].append(
+                start(whole.at[me], whole.at[me], chunks[c][12].at[step - 1], (2 * far_chip + core, wa, ba))
+            )
+
+    def relay(c):
+        whole = chunks[c][7]
+        for copy in flying[c]:
+            copy.wait()
+        held = pl.ds(wa * chips, chips)
+        flying[c] = [start(whole.at[held], whole.at[held], chunks[c][12].at[chips - 1], side)]
+
     def mirror(c):
         whole, core_all = chunks[c][7:9]
         for copy in flying[c]:
             copy.wait()
         flying[c] = start(whole, core_all, chunks[c][13], partner)
-        put(c, whole, core)
 
     def finish(c):
+        put(c, chunks[c][7], core)
         flying[c].wait()
         put(c, chunks[c][8], 1 - core)
 
+    unit = lanes // 2
+    proj_at = 3 * depth // 2
+
+    targets_of = [
+        [(proj_at + k * unit, proj_at + (1 + k) * unit) for k in range(2)],
+        [(k * unit, (3 + k) * unit) for k in range(2)],
+        [((4 + k) * unit, (1 + k if k < 2 else 5 + k) * unit) for k in range(4)],
+        [(2 * unit, 5 * unit), (3 * unit, 6 * unit), (8 * unit, 0), (proj_at + 2 * unit, proj_at)],
+    ]
+
     def put(c, source, which):
         r = source.shape[1]
-        w = peers * r
-        begin_rows = half_starts[c]
-        step_rows = lanes // 2
-        for first in range(0, 2 * w, step_rows):
-            near, away = begin_rows[first // step_rows]
-            for j in range(first % w // r, min(peers, (first % w + step_rows) // r)):
-                inside = j * r - first % w
-
-                def one(is_wq, near_row, away_row, out):
-                    row = jnp.where(ba == 0, near_row, away_row) + inside
-                    out[pl.ds(pl.multiple_of(row, 8), r), :] = source[j].astype(f32)
-
-                @pl.when(which == first // w)
-                def _():
-                    one(near[0], near[1], away[1], near[0])
-
-    unit = lanes // 2
-    half_starts = [
-        [((wp_out, k * unit), (wp_out, (1 + k) * unit)) for k in range(2)],
-        [((wq_out, k * unit), (wq_out, (3 + k) * unit)) for k in range(2)],
-        [((wq_out, (4 + k) * unit), (wq_out, (1 + k if k < 2 else 5 + k) * unit)) for k in range(4)],
-        [
-            ((wq_out, 2 * unit), (wq_out, 5 * unit)), ((wq_out, 3 * unit), (wq_out, 6 * unit)),
-            ((wq_out, 8 * unit), (wq_out, 0)), ((wp_out, 2 * unit), (wp_out, 0)),
-        ],
-    ]
-
-    product = mxu(d_proj, att_ref[...], TN)
+        blocks = peers * r // unit
+        for k in range(blocks):
+            zero, one = targets_of[c][k], targets_of[c][blocks + k]
+            row = jnp.where(
+                which == 0, jnp.where(ba == 0, zero[0], zero[1]), jnp.where(ba == 0, one[0], one[1])
+            )
+            for j in range(unit // r):
+                grads_out[pl.ds(pl.multiple_of(row + j * r, 8), r), :] = source[k * (unit // r) + j].astype(f32)
+
+    product = mxu(d_proj_ref[...], att_ref[...], TN)
     product_ref[:lanes] = product[:lanes]
     p_mid[...] = product[lanes : 2 * lanes]
     product_ref[lanes : 2 * lanes] = product[2 * lanes :]
     begin(0)
-    d_att_ref[...] = mxu(d_proj, w_proj_ref[...], NT).astype(b16)
-
-    def backward_group(g):
+
+    def backward_group(g, between=None):
         def backward(step, total):
             units = [step * BWD + k for k in range(BWD)]
             grads = []
@@ -739,7 +783,11 @@
             return total
 
         d_bias_ref[g] = jnp.zeros((length, wide), f32)
-        lax.fori_loop(0, count // BWD, backward, 0)
+        cut_at = count // BWD // 2 if between else count // BWD
+        lax.fori_loop(0, cut_at, backward, 0)
+        if between:
+            between()
+            lax.fori_loop(cut_at, count // BWD, backward, 0)
         for part, ref in enumerate((raw_q_ref, raw_k_ref)):
             place = slice(part * depth + g * lanes, part * depth + (g + 1) * lanes)
             value, grad = qkv_ref[:, place].astype(f32), ref[...]
@@ -753,33 +801,37 @@
                 grad - value * norm_ref[part, g] * mxu_fine(along, lane_lane, NN)
             ).astype(b16)
 
-    def dense_column(row, part, g, rows_from=0, rows_to=None):
-        place = slice(part * depth + g * lanes, part * depth + (g + 1) * lanes)
-        product_ref[row : row + lanes] = mxu(d_qkv_ref[:, place], flat_ref[...], TN)
-
+    def dense(g):
+        joined = jnp.concatenate(
+            [d_qkv_ref[:, part * depth + g * lanes : part * depth + (g + 1) * lanes] for part in range(3)], 1
+        )
+        return mxu(joined, flat_ref[...], TN)
+
+    norms(early, count)
     backward_group(0)
-    dense_column(0, 0, 0)
-    dense_column(lanes, 2, 0)
+    product = dense(0)
+    product_ref[:lanes] = product[:lanes]
+    product_ref[lanes : 2 * lanes] = product[2 * lanes :]
+    k_first[...] = product[lanes : 2 * lanes]
     begin(1)
     cross(0)
-    backward_group(2)
-    dense_column(0, 0, 2)
-    dense_column(lanes, 1, 0)
-    dense_column(2 * lanes, 1, 2)
-    dense_column(3 * lanes, 2, 2)
+    backward_group(2, lambda: cross(1))
+    product = dense(2)
+    product_ref[:lanes] = product[:lanes]
+    product_ref[lanes : 2 * lanes] = k_first[...]
+    product_ref[2 * lanes : 4 * lanes] = product[lanes:]
     begin(2)
-    cross(1)
-    backward_group(1)
-    dense_column(0, 0, 1)
-    dense_column(2 * lanes, 2, 1)
-    key = mxu(d_qkv_ref[:, depth + lanes : depth + 2 * lanes], flat_ref[...], TN)
-    product_ref[lanes : lanes + unit] = key[:unit]
+    scatter(0)
+    backward_group(1, lambda: cross(2))
+    product = dense(1)
+    product_ref[:lanes] = product[:lanes]
+    product_ref[lanes : lanes + unit] = product[lanes : lanes + unit]
     product_ref[lanes + unit : 2 * lanes] = p_mid[:unit]
-    product_ref[3 * lanes : 3 * lanes + unit] = key[unit:]
+    product_ref[2 * lanes : 3 * lanes] = product[2 * lanes :]
+    product_ref[3 * lanes : 3 * lanes + unit] = product[lanes + unit : 2 * lanes]
     product_ref[3 * lanes + unit : 4 * lanes] = p_mid[unit:]
     begin(3)
-    scatter(0)
-    cross(2)
+    scatter(1)
     d_flat_ref[...] = mxu(d_qkv_ref[...], w_qkv_ref[...], NT).astype(b16)
 
     def back_tiles(i):
@@ -802,46 +854,63 @@
         start(col_back.at[pl.ds(far, cut // 2)], diag_back_get, back_sems.at[2], (below, right, ba)),
     ]
     cross(3)
+    spread_column(0)
     for k, row in enumerate(fold_bias([d_bias_ref[g] for g in range(groups)], length, window, span)):
         small[k : k + 1, :] = row
     tiny = start(small, small_core, tiny_sems.at[0], partner)
-    scatter(1)
-    gather(0)
-    tiny.wait()
-    small_a[...] = small[...] + small_core[...]
-    tiny = start(small_a, small_image, tiny_sems.at[1], image)
-    scatter(2)
-    tiny.wait()
-    small_b[...] = small_a[...] + small_image[...]
-    tinies = []
-    for step in range(1, peers):
-        tinies.append(start(small_b, small_near.at[step - 1], tiny_sems.at[step + 1], peer(step)[1]))
 
     def put_row(i, turned, edge, odd):
         ahead = [half_turn(edge, 0) if odd else edge] + turned
         out = [jnp.where(low_sub, ahead[k], ahead[k + 1]) for k in range(across)]
         d_tok_ref[i] = (jnp.concatenate(out, 0) + cot[i].astype(f32)).astype(b16)
 
+    scatter(2)
     back[1].wait()
     for i in range(rows - cut):
         put_row(i + cut, back_tiles(i), col_back_get[i // 2].astype(f32), i % 2 == 1)
-    gather(1)
-    scatter(3)
+    spread_column(1)
+    tiny.wait()
+    small_half = small_a.shape[0]
+    my_rows = pl.ds(pl.multiple_of(core * small_half, 8), small_half)
+    small_a[...] = small[my_rows, :] + small_core[my_rows, :]
+    tiny = start(small_a, small_image, tiny_sems.at[1], image)
+    relay(0)
     back[0].wait()
     back[2].wait()
     for i in range(cut):
         whole_row = row_back_get[i].astype(f32)
         turned = [whole_row[k * window : (k + 1) * window] for k in range(across)]
         put_row(i, turned, diag_back_get[i // 2].astype(f32), i % 2 == 1)
-    gather(2)
+    scatter(3)
+    tiny.wait()
+    small_b[...] = small_a[...] + small_image[...]
+    tiny = start(small_b, small_side, tiny_sems.at[2], side)
+    spread_column(2)
     mirror(0)
+    relay(1)
+    tiny.wait()
+    small_c[...] = small_b[...] + small_side[...]
+    tinies = []
+    for step in range(1, chips):
+        far_chip = lax.rem(ha // 2 + step, chips)
+        tinies.append(
+            start(small_c, small_near.at[step - 1], tiny_sems.at[step + 2], (2 * far_chip + core, wa, ba))
+        )
+    finish(0)
+    gather(3)
+    relay(2)
     mirror(1)
-    gather(3)
     for copy in tinies:
         copy.wait()
-    total = small_b[...]
-    for step in range(1, peers):
+    total = small_c[...]
+    for step in range(1, chips):
         total = total + small_near[step - 1]
+    small_total[my_rows, :] = total
+    tiny = start(small_total.at[my_rows], small_total.at[my_rows], tiny_sems.at[chips + 2], partner)
+    finish(1)
+    mirror(2)
+    tiny.wait()
+    total = small_total[...]
     table_out[...] = (total[: head_rows] * (BIAS_RANGE * sigma * (1.0 - sigma)))[:heads, :entries]
     gain_row = jnp.concatenate([total[heads : heads + 1, :], total[heads + 1 : heads + 2, : depth - span]], 1)
     gain_out[...] = gain_row.reshape(depth)
@@ -852,18 +921,18 @@
     for h in range(heads):
         logits = jnp.where(at == h, scale_ref[h], logits)
     scale_out[...] = jnp.where(logits < SCALE_CAP, sums, 0.0).reshape(128)[:heads]
-    finish(0)
-    finish(1)
-    mirror(2)
+    mirror(3)
     finish(2)
-    mirror(3)
     finish(3)
 
 
-def finish_kernel(*refs):
-    count = len(refs) // 2
-    sems = refs[-1]
-    copies = [pltpu.make_async_copy(refs[k], refs[count + k], sems.at[k]) for k in range(count)]
+def finish_kernel(tok_ref, grads_ref, table_ref, scale_ref, gain_ref, tok, wq, wp, table, scale, gain, sems):
+    cut = wq.shape[0]
+    pairs = (
+        (grads_ref.at[pl.ds(0, cut)], wq), (grads_ref.at[pl.ds(cut, wp.shape[0])], wp), (tok_ref, tok),
+        (table_ref, table), (scale_ref, scale), (gain_ref, gain),
+    )
+    copies = [pltpu.make_async_copy(src, dst, sems.at[k]) for k, (src, dst) in enumerate(pairs)]
     for copy in copies:
         copy.start()
     for copy in copies:
@@ -899,7 +968,7 @@
             vmem((peers, r, depth), b16), vmem((peers, r, depth), b16),
             dma((2,)), dma((3, 2)), dma((chips - 1, 2)), dma((peers - 1, 2)), dma((2,)),
         ]
-    small = (16, span)
+    small, part = (16, span), (8, span)
     anywhere = pl.BlockSpec(memory_space=pltpu.HBM)
     pinned = [
         pltpu.with_memory_space_constraint(x, pltpu.HBM)
@@ -909,30 +978,30 @@
         functools.partial(whole_kernel, (size_h, size_w), height, width, window),
         out_shape=[
             jax.ShapeDtypeStruct((rows, cols, depth), b16),
-            jax.ShapeDtypeStruct((3 * depth // 2, depth), f32),
-            jax.ShapeDtypeStruct((depth // 2, depth), f32),
+            jax.ShapeDtypeStruct((2 * depth, depth), f32),
             jax.ShapeDtypeStruct((heads, entries), f32),
             jax.ShapeDtypeStruct((heads,), f32),
             jax.ShapeDtypeStruct((depth,), f32),
         ],
         in_specs=[anywhere] * 6 + [pl.BlockSpec(memory_space=pltpu.SMEM)],
-        out_specs=[VMEM] * 6,
+        out_specs=[VMEM] * 5,
         scratch_shapes=[
             vmem((rows, cols, depth), b16), vmem((rows, cols, depth), b16),
             vmem((depth, 3 * depth), b16), vmem((depth, depth), b16),
             vmem((heads, entries), f32), vmem((depth,), f32), vmem((head_rows, span), f32), dma((6,)),
             vmem((2, rows // 2, window, depth), b16), vmem((2, cut, cols, depth), b16),
             vmem((2, rows // 2, window, depth), b16), vmem((2, cut // 2, window, depth), b16), dma((2, 3, 2)),
-            vmem((total, depth), b16), vmem((total, depth), b16), vmem((total, depth), b16),
+            vmem((total, depth), b16), vmem((total, depth), b16), vmem((total, depth), b16), vmem((total, depth), b16),
             vmem((total, 3 * depth), b16), vmem((total, depth), b16), vmem((total, depth), b16),
             vmem((total, 3 * depth), b16), vmem((count, groups, length, wide), f32), vmem((groups, total, wide), f32),
             vmem((count, groups, 1, wide), f32), vmem((4, groups, length, wide), f32),
             vmem((total, lanes), f32), vmem((total, lanes), f32), vmem((2, groups, total, lanes), f32),
-            vmem((groups, length, wide), f32), vmem((lanes, depth), f32), vmem((4 * lanes, depth), f32),
+            vmem((groups, length, wide), f32), vmem((lanes, depth), f32), vmem((lanes, depth), f32),
+            vmem((4 * lanes, depth), f32),
             vmem((cut, cols, depth), b16), vmem((rows // 2, window, depth), b16), vmem((cut, cols, depth), b16),
             vmem(((rows - cut) // 2, window, depth), b16), vmem((cut // 2, window, depth), b16), dma((3, 2)),
-            vmem(small, f32), vmem(small, f32), vmem(small, f32), vmem(small, f32), vmem(small, f32),
-            vmem((peers - 1, *small), f32), dma((peers + 1, 2)),
+            vmem(small, f32), vmem(small, f32), vmem(part, f32), vmem(part, f32), vmem(part, f32), vmem(part, f32),
+            vmem(part, f32), vmem((chips - 1, *part), f32), vmem(small, f32), dma((chips + 3, 2)),
             *chunk_scratch,
         ],
         compiler_params=pltpu.CompilerParams(
@@ -942,8 +1011,15 @@
     )(*pinned, logit_scale)
     d_tok, half_qkv, half_proj, d_table, d_scale, d_gain = pl.pallas_call(
         finish_kernel,
-        out_shape=[jax.ShapeDtypeStruct(x.shape, x.dtype) for x in outs],
-        in_specs=[VMEM] * 6,
+        out_shape=[
+            jax.ShapeDtypeStruct((rows, cols, depth), b16),
+            jax.ShapeDtypeStruct((3 * depth // 2, depth), f32),
+            jax.ShapeDtypeStruct((depth // 2, depth), f32),
+            jax.ShapeDtypeStruct((heads, entries), f32),
+            jax.ShapeDtypeStruct((heads,), f32),
+            jax.ShapeDtypeStruct((depth,), f32),
+        ],
+        in_specs=[VMEM] * 5,
         out_specs=[anywhere] * 6,
         scratch_shapes=[dma((6,))],
         compiler_params=pltpu.CompilerParams(vmem_limit_bytes=FINISH_LIMIT),
@@ -959,7 +1035,7 @@
     return (
         images == 1 and size_b == 2 and size_w == 2 and size_h % 2 == 0 and size_h > 2
         and logit_scale.shape[0] == 3 * GROUP and depth == 3 * 128 and WIN == 8
-        and rows % WIN == 0 and cols % (2 * WIN) == 0 and rows * cols // 64 % BWD == 0
+        and rows % WIN == 0 and cols % (2 * WIN) == 0 and rows * cols // 64 % (2 * BWD) == 0 and rows > WIN
         and 64 % peers == 0 and 64 // peers % 8 == 0
     )
 

time: 46.3 us -> 43.6 us (0.942)
  Pallas kernels: 44.8 us -> 42.1 us
    pallas_call x1, Pallas kernels: 43.6 us -> 40.9 us  [whole_grads(): pl.pallas_call(functools.partial(whole_kernel, (size_h, size_w), height,...]
where the time goes in v3:
time: 43.6 us; the launch traced here: 43.4 us
  Pallas kernels  42.1 us (97%)
  local copies, waits for them, and re-layouts  0.65 us (1%)
  between operations  0.65 us (1%)
    pallas_call x1, Pallas kernels, whole_grads(): pl.pallas_call(functools.partial(whole_kernel, (size_h, size_w), height,...  40.9 us
    pallas_call x1, Pallas kernels, whole_grads(): pl.pallas_call(finish_kernel, out_shape=[jax.ShapeDtypeStruct((rows, cols...  1.2 us

profile of v3, /device:TPU:0, one launch (start us, length us, event | category | flops | bytes accessed | tf_op | source)
XLA Modules:
  0.0 43.4 jit_solution(7516721008105778274)
XLA Ops:
  0.6 0.0 copy-start
  0.6 0.6 %copy-done = f32[12]{0:T(128)S(1)} copy-done((f32[12]{0:T(128)S(1)}, f32[12]{0:T(128)}, u32[]{:S(2)}) %copy-start) | copy-done | bytes 72
  1.3 40.9 %whole_grads.1 = (bf16[16,32,384]{2,1,0:T(8,128)(2,1)S(1)}, f32[768,384]{1,0:T(8,128)S(1)}, f32[12,225]{1,0:T(8,128)S(1)}, f32[12]{0:T(128)S(1)}, f32[384]{0:T(512)S(1)}) custom-call(bf16[1,16,32,384]{3,2,1,0:T(8,128)(2,1)} %tokens_ref.1, bf16[1,16,32,384]{3,2,1,0:T(8,128)(2,1)} %cot_ref.1, bf16[384,1152]{1,0:T(8,128)(2,1)} %w_qkv_hbm.1, ...), custom_call_target="tpu_custom_call" | custom-call | tf_op jit(solution)/shard_map/whole_grads/pallas_call | solution.py:977
  42.2 1.2 %finish.1 = (bf16[16,32,384]{2,1,0:T(8,128)(2,1)}, f32[576,384]{1,0:T(8,128)}, f32[192,384]{1,0:T(8,128)}, f32[12,225]{1,0:T(8,128)}, f32[12]{0:T(128)}, /*index=5*/f32[384]{0:T(512)}) custom-call(bf16[16,32,384]{2,1,0:T(8,128)(2,1)S(1)} %get-tuple-element.17.tok_ref, f32[768,384]{1,0:T(8,128)S(1)} %get-tuple-element.18.grads_ref, ...), custom_call_target="tpu_custom_call" | custom-call | tf_op jit(solution)/shard_map/finish/pallas_call | solution.py:1012
Async XLA Ops:
  0.6 0.7 %copy-start = (f32[12]{0:T(128)S(1)}, f32[12]{0:T(128)}, u32[]{:S(2)}) copy-start(f32[12]{0:T(128)} %scale_ref.1) | copy-start | bytes 148

commit v4 on v3

--- a/solution.py
+++ b/solution.py
@@ -452,6 +452,12 @@
         copy.start()
         return copy
 
+    def all_of(src, dst, sems, device):
+        return pltpu.make_async_remote_copy(
+            src_ref=src, dst_ref=dst, send_sem=sems.at[0], recv_sem=sems.at[1],
+            device_id=device, device_id_type=MESH,
+        )
+
     rows, cols, depth = tok.shape
     cut = window // 2
     length = window * window
@@ -654,11 +660,11 @@
         flying[c].wait()
         core_mine[...] = core_mine[...] + core_get[...].astype(f32)
         w = plane_send.shape[1]
-        flying[c] = []
         for k, (b, y, device) in enumerate(((1 - ba, wa, image), (ba, 1 - wa, side), (1 - ba, 1 - wa, corner))):
             place = pl.ds(pl.multiple_of((2 * b + y) * w, 32), w)
             plane_send[k] = core_mine[place, :].astype(b16)
-            flying[c].append(start(plane_send.at[k], plane_get.at[k], chunks[c][10].at[k], device))
+            start(plane_send.at[k], plane_get.at[k], chunks[c][10], device)
+        flying[c] = [all_of(plane_send, plane_get, chunks[c][10], image)]
 
     def scatter(c):
         core_mine, plane_get, near_send, near_get = chunks[c][1], chunks[c][4], chunks[c][5], chunks[c][6]
@@ -671,15 +677,10 @@
         r = near_send.shape[1]
         for j in range(chips):
             near_send[j] = total[j * r : (j + 1) * r].astype(b16)
-        flying[c] = []
         for step in range(1, chips):
             far_chip = lax.rem(ha // 2 + step, chips)
-            flying[c].append(
-                start(
-                    near_send.at[far_chip], near_get.at[step - 1], chunks[c][11].at[step - 1],
-                    (2 * far_chip + core, wa, ba),
-                )
-            )
+            start(near_send.at[far_chip], near_get.at[step - 1], chunks[c][11], (2 * far_chip + core, wa, ba))
+        flying[c] = [all_of(near_send.at[pl.ds(0, chips - 1)], near_get, chunks[c][11], partner)]
 
     def gather(c):
         near_send, near_get, whole = chunks[c][5:8]
@@ -689,9 +690,10 @@
         for step in range(1, chips):
             total = total + near_get[step - 1].astype(f32)
         whole[me] = total.astype(b16)
-        flying[c] = []
         for step in range(1, peers):
-            flying[c].append(start(whole.at[me], whole.at[me], chunks[c][12].at[step - 1], peer(step)[1]))
+            start(whole.at[me], whole.at[me], chunks[c][12], peer(step)[1])
+        several = whole.at[pl.ds(0, peers - 1)]
+        flying[c] = [all_of(several, several, chunks[c][12], partner)]
 
     def spread_column(c):
         near_send, near_get, whole = chunks[c][5:8]
@@ -701,19 +703,18 @@
         for step in range(1, chips):
             total = total + near_get[step - 1].astype(f32)
         whole[me] = total.astype(b16)
-        flying[c] = []
         for step in range(1, chips):
             far_chip = lax.rem(ha // 2 + step, chips)
-            flying[c].append(
-                start(whole.at[me], whole.at[me], chunks[c][12].at[step - 1], (2 * far_chip + core, wa, ba))
-            )
+            start(whole.at[me], whole.at[me], chunks[c][12], (2 * far_chip + core, wa, ba))
+        several = whole.at[pl.ds(0, chips - 1)]
+        flying[c] = [all_of(several, several, chunks[c][12], partner)]
 
     def relay(c):
         whole = chunks[c][7]
         for copy in flying[c]:
             copy.wait()
         held = pl.ds(wa * chips, chips)
-        flying[c] = [start(whole.at[held], whole.at[held], chunks[c][12].at[chips - 1], side)]
+        flying[c] = [start(whole.at[held], whole.at[held], chunks[c][14], side)]
 
     def mirror(c):
         whole, core_all = chunks[c][7:9]
@@ -753,7 +754,7 @@
     product_ref[lanes : 2 * lanes] = product[2 * lanes :]
     begin(0)
 
-    def backward_group(g, between=None):
+    def backward_group(g):
         def backward(step, total):
             units = [step * BWD + k for k in range(BWD)]
             grads = []
@@ -783,11 +784,7 @@
             return total
 
         d_bias_ref[g] = jnp.zeros((length, wide), f32)
-        cut_at = count // BWD // 2 if between else count // BWD
-        lax.fori_loop(0, cut_at, backward, 0)
-        if between:
-            between()
-            lax.fori_loop(cut_at, count // BWD, backward, 0)
+        lax.fori_loop(0, count // BWD, backward, 0)
         for part, ref in enumerate((raw_q_ref, raw_k_ref)):
             place = slice(part * depth + g * lanes, part * depth + (g + 1) * lanes)
             value, grad = qkv_ref[:, place].astype(f32), ref[...]
@@ -815,14 +812,16 @@
     k_first[...] = product[lanes : 2 * lanes]
     begin(1)
     cross(0)
-    backward_group(2, lambda: cross(1))
+    backward_group(2)
+    cross(1)
     product = dense(2)
     product_ref[:lanes] = product[:lanes]
     product_ref[lanes : 2 * lanes] = k_first[...]
     product_ref[2 * lanes : 4 * lanes] = product[lanes:]
     begin(2)
     scatter(0)
-    backward_group(1, lambda: cross(2))
+    backward_group(1)
+    cross(2)
     product = dense(1)
     product_ref[:lanes] = product[:lanes]
     product_ref[lanes : lanes + unit] = product[lanes : lanes + unit]
@@ -890,12 +889,10 @@
     relay(1)
     tiny.wait()
     small_c[...] = small_b[...] + small_side[...]
-    tinies = []
     for step in range(1, chips):
         far_chip = lax.rem(ha // 2 + step, chips)
-        tinies.append(
-            start(small_c, small_near.at[step - 1], tiny_sems.at[step + 2], (2 * far_chip + core, wa, ba))
-        )
+        start(small_c, small_near.at[step - 1], tiny_sems.at[3], (2 * far_chip + core, wa, ba))
+    tinies = [all_of(small_near, small_near, tiny_sems.at[3], partner)]
     finish(0)
     gather(3)
     relay(2)
@@ -906,7 +903,7 @@
     for step in range(1, chips):
         total = total + small_near[step - 1]
     small_total[my_rows, :] = total
-    tiny = start(small_total.at[my_rows], small_total.at[my_rows], tiny_sems.at[chips + 2], partner)
+    tiny = start(small_total.at[my_rows], small_total.at[my_rows], tiny_sems.at[4], partner)
     finish(1)
     mirror(2)
     tiny.wait()
@@ -966,7 +963,7 @@
             vmem((3, w // 2, depth), b16), vmem((3, w // 2, depth), b16),
             vmem((chips, r, depth), b16), vmem((chips - 1, r, depth), b16),
             vmem((peers, r, depth), b16), vmem((peers, r, depth), b16),
-            dma((2,)), dma((3, 2)), dma((chips - 1, 2)), dma((peers - 1, 2)), dma((2,)),
+            dma((2,)), dma((2,)), dma((2,)), dma((2,)), dma((2,)), dma((2,)),
         ]
     small, part = (16, span), (8, span)
     anywhere = pl.BlockSpec(memory_space=pltpu.HBM)
@@ -1001,7 +998,7 @@
             vmem((cut, cols, depth), b16), vmem((rows // 2, window, depth), b16), vmem((cut, cols, depth), b16),
             vmem(((rows - cut) // 2, window, depth), b16), vmem((cut // 2, window, depth), b16), dma((3, 2)),
             vmem(small, f32), vmem(small, f32), vmem(part, f32), vmem(part, f32), vmem(part, f32), vmem(part, f32),
-            vmem(part, f32), vmem((chips - 1, *part), f32), vmem(small, f32), dma((chips + 3, 2)),
+            vmem(part, f32), vmem((chips - 1, *part), f32), vmem(small, f32), dma((5, 2)),
             *chunk_scratch,
         ],
         compiler_params=pltpu.CompilerParams(

time: 43.6 us -> 43.1 us (0.989)
    pallas_call x1, Pallas kernels: 40.9 us -> 40.5 us  [whole_grads(): pl.pallas_call(functools.partial(whole_kernel, (size_h, size_w), height,...]
where the time goes in v4:
time: 43.1 us; the launch traced here: 43 us
  Pallas kernels  41.7 us (97%)
  local copies, waits for them, and re-layouts  0.65 us (2%)
  between operations  0.65 us (2%)
    pallas_call x1, Pallas kernels, whole_grads(): pl.pallas_call(functools.partial(whole_kernel, (size_h, size_w), height,...  40.5 us
    pallas_call x1, Pallas kernels, whole_grads(): pl.pallas_call(finish_kernel, out_shape=[jax.ShapeDtypeStruct((rows, cols...  1.2 us

profile of v4, /device:TPU:0, one launch (start us, length us, event | category | flops | bytes accessed | tf_op | source)
XLA Modules:
  0.0 43.0 jit_solution(15631549849511945616)
XLA Ops:
  0.6 0.0 copy-start
  0.6 0.6 %copy-done = f32[12]{0:T(128)S(1)} copy-done((f32[12]{0:T(128)S(1)}, f32[12]{0:T(128)}, u32[]{:S(2)}) %copy-start) | copy-done | bytes 72
  1.3 40.5 %whole_grads.1 = (bf16[16,32,384]{2,1,0:T(8,128)(2,1)S(1)}, f32[768,384]{1,0:T(8,128)S(1)}, f32[12,225]{1,0:T(8,128)S(1)}, f32[12]{0:T(128)S(1)}, f32[384]{0:T(512)S(1)}) custom-call(bf16[1,16,32,384]{3,2,1,0:T(8,128)(2,1)} %tokens_ref.1, bf16[1,16,32,384]{3,2,1,0:T(8,128)(2,1)} %cot_ref.1, bf16[384,1152]{1,0:T(8,128)(2,1)} %w_qkv_hbm.1, ...), custom_call_target="tpu_custom_call" | custom-call | tf_op jit(solution)/shard_map/whole_grads/pallas_call | solution.py:974
  41.8 1.2 %finish.1 = (bf16[16,32,384]{2,1,0:T(8,128)(2,1)}, f32[576,384]{1,0:T(8,128)}, f32[192,384]{1,0:T(8,128)}, f32[12,225]{1,0:T(8,128)}, f32[12]{0:T(128)}, /*index=5*/f32[384]{0:T(512)}) custom-call(bf16[16,32,384]{2,1,0:T(8,128)(2,1)S(1)} %get-tuple-element.17.tok_ref, f32[768,384]{1,0:T(8,128)S(1)} %get-tuple-element.18.grads_ref, ...), custom_call_target="tpu_custom_call" | custom-call | tf_op jit(solution)/shard_map/finish/pallas_call | solution.py:1009
Async XLA Ops:
  0.6 0.7 %copy-start = (f32[12]{0:T(128)S(1)}, f32[12]{0:T(128)}, u32[]{:S(2)}) copy-start(f32[12]{0:T(128)} %scale_ref.1) | copy-start | bytes 148

commit v5 on v4

--- a/solution.py
+++ b/solution.py
@@ -46,6 +46,8 @@
 GROUP = 4
 FWD = 2
 BWD = 4
+LONG_FWD = 4
+LONG_BWD = 8
 LOG2E = math.log2(math.e)
 VMEM_LIMIT = 40 * 2**20
 FINISH_LIMIT = 4 * 2**20
@@ -399,9 +401,9 @@
 
 def whole_kernel(
     shape, height, width, window,
-    tokens_ref, cot_ref, w_qkv_hbm, w_proj_hbm, table_hbm, gain_hbm, scale_ref,
+    tokens_ref, cot_ref, w_qkv_hbm, w_proj_hbm, table_hbm, gain_hbm, scale_hbm,
     d_tok_ref, grads_out, table_out, scale_out, gain_out,
-    tok, cot, w_qkv_ref, w_proj_ref, table_in, gain_ref, table_ref, local_sems,
+    tok, cot, w_qkv_ref, w_proj_ref, table_in, gain_ref, scale_ref, table_ref, local_sems,
     col_send, row_get, col_get, diag_get, halo_sems,
     flat_ref, grad_ref, d_flat_ref, d_proj_ref,
     qkv_ref, att_ref, d_att_ref, d_qkv_ref, probs_ref, kinv_ref, qrow_ref, masked_ref, raw_q_ref, raw_k_ref,
@@ -430,7 +432,7 @@
     for k, (src, dst) in enumerate(
         (
             (tokens_ref.at[0], tok), (cot_ref.at[0], cot), (w_qkv_hbm, w_qkv_ref), (w_proj_hbm, w_proj_ref),
-            (table_hbm, table_in), (gain_hbm, gain_ref),
+            (table_hbm, table_in), (gain_hbm, gain_ref), (scale_hbm, scale_ref),
         )
     ):
         copy = pltpu.make_async_copy(src, dst, local_sems.at[k])
@@ -463,6 +465,7 @@
     length = window * window
     across = cols // window
     count = rows // window * across
+    fwd, bwd = math.gcd(across, LONG_FWD), math.gcd(count, LONG_BWD)
     tokens = count * length
     groups = qrow_ref.shape[1]
     lanes = depth // groups
@@ -492,8 +495,8 @@
     pack_columns(1, cot)
     send_halo(1, cot)
 
-    loads[4].wait()
-    loads[5].wait()
+    for k in range(4, 7):
+        loads[k].wait()
     heads = groups * GROUP
     entries = table_in.shape[1]
     table_ref[...] = jnp.zeros_like(table_ref)
@@ -567,9 +570,8 @@
             for part in range(2):
                 place = slice(part * depth + g * lanes, part * depth + (g + 1) * lanes)
                 high, low = split(jnp.square(qkv_ref[part_rows, place].astype(f32)))
-                norm_ref[part, g, part_rows] = 1.0 / (
-                    mxu(high, lane_lane, NN) + mxu(low, lane_lane, NN) + 1.0
-                )
+                inv = lax.rsqrt(mxu(high, lane_lane, NN) + mxu(low, lane_lane, NN) + 1.0)
+                norm_ref[part, g, part_rows] = inv * inv
 
     def load(ref, w, g, part):
         return ref[
@@ -578,7 +580,7 @@
         ]
 
     def forward(step, carry):
-        units = [(step * FWD + k, g) for k in range(FWD) for g in range(groups)]
+        units = [(step * fwd + k, g) for k in range(fwd) for g in range(groups)]
         scores = []
         for w, g in units:
             query, key = load(qkv_ref, w, g, 0), load(qkv_ref, w, g, 1)
@@ -621,7 +623,7 @@
     gather_rows(0, tok, flat_ref, 0, rows - window)
     loads[2].wait()
     project(0, early)
-    lax.fori_loop(0, early // FWD, forward, 0)
+    lax.fori_loop(0, early // fwd, forward, 0)
     norms(0, early)
     halos[1, 0].wait()
     gather_rows(1, cot, grad_ref, 0, rows - window)
@@ -631,7 +633,7 @@
     halos[0, 2].wait()
     gather_rows(0, tok, flat_ref, rows - window, rows)
     project(early, count)
-    lax.fori_loop(early // FWD, count // FWD, forward, 0)
+    lax.fori_loop(early // fwd, count // fwd, forward, 0)
     halos[1, 1].wait()
     halos[1, 2].wait()
     gather_rows(1, cot, grad_ref, rows - window, rows)
@@ -756,7 +758,7 @@
 
     def backward_group(g):
         def backward(step, total):
-            units = [step * BWD + k for k in range(BWD)]
+            units = [step * bwd + k for k in range(bwd)]
             grads = []
             for w in units:
                 d_tall = tile_heads(load(d_att_ref, w, g, 0), head_dim)
@@ -784,7 +786,7 @@
             return total
 
         d_bias_ref[g] = jnp.zeros((length, wide), f32)
-        lax.fori_loop(0, count // BWD, backward, 0)
+        lax.fori_loop(0, count // bwd, backward, 0)
         for part, ref in enumerate((raw_q_ref, raw_k_ref)):
             place = slice(part * depth + g * lanes, part * depth + (g + 1) * lanes)
             value, grad = qkv_ref[:, place].astype(f32), ref[...]
@@ -969,7 +971,7 @@
     anywhere = pl.BlockSpec(memory_space=pltpu.HBM)
     pinned = [
         pltpu.with_memory_space_constraint(x, pltpu.HBM)
-        for x in (tokens, cotangent, w_qkv, w_proj, table_logits, gain)
+        for x in (tokens, cotangent, w_qkv, w_proj, table_logits, gain, logit_scale)
     ]
     outs = pl.pallas_call(
         functools.partial(whole_kernel, (size_h, size_w), height, width, window),
@@ -980,12 +982,13 @@
             jax.ShapeDtypeStruct((heads,), f32),
             jax.ShapeDtypeStruct((depth,), f32),
         ],
-        in_specs=[anywhere] * 6 + [pl.BlockSpec(memory_space=pltpu.SMEM)],
+        in_specs=[anywhere] * 7,
         out_specs=[VMEM] * 5,
         scratch_shapes=[
             vmem((rows, cols, depth), b16), vmem((rows, cols, depth), b16),
             vmem((depth, 3 * depth), b16), vmem((depth, depth), b16),
-            vmem((heads, entries), f32), vmem((depth,), f32), vmem((head_rows, span), f32), dma((6,)),
+            vmem((heads, entries), f32), vmem((depth,), f32), pltpu.SMEM((heads,), f32),
+            vmem((head_rows, span), f32), dma((7,)),
             vmem((2, rows // 2, window, depth), b16), vmem((2, cut, cols, depth), b16),
             vmem((2, rows // 2, window, depth), b16), vmem((2, cut // 2, window, depth), b16), dma((2, 3, 2)),
             vmem((total, depth), b16), vmem((total, depth), b16), vmem((total, depth), b16), vmem((total, depth), b16),
@@ -1005,7 +1008,7 @@
             collective_id=0, has_side_effects=True, vmem_limit_bytes=VMEM_LIMIT
         ),
         name="whole_grads",
-    )(*pinned, logit_scale)
+    )(*pinned)
     d_tok, half_qkv, half_proj, d_table, d_scale, d_gain = pl.pallas_call(
         finish_kernel,
         out_shape=[
@@ -1032,7 +1035,7 @@
     return (
         images == 1 and size_b == 2 and size_w == 2 and size_h % 2 == 0 and size_h > 2
         and logit_scale.shape[0] == 3 * GROUP and depth == 3 * 128 and WIN == 8
-        and rows % WIN == 0 and cols % (2 * WIN) == 0 and rows * cols // 64 % (2 * BWD) == 0 and rows > WIN
+        and rows % WIN == 0 and cols % (2 * WIN) == 0 and rows > WIN
         and 64 % peers == 0 and 64 // peers % 8 == 0
     )
 

time: 43.1 us -> 39.9 us (0.926)
  Pallas kernels: 41.7 us -> 39.1 us
  local copies, waits for them, and re-layouts: 0.65 us -> 0 us
    pallas_call x1, Pallas kernels: 40.5 us -> 37.9 us  [whole_grads(): pl.pallas_call(functools.partial(whole_kernel, (size_h, size_w), height,...]
    unnamed x2 -> x0, local copies, waits for them, and re-layouts: 0.65 us -> none
where the time goes in v5:
time: 39.9 us; the launch traced here: 39.8 us
  Pallas kernels  39.1 us (98%)
  between operations  0.64 us (2%)
    pallas_call x1, Pallas kernels, whole_grads(): pl.pallas_call(functools.partial(whole_kernel, (size_h, size_w), height,...  37.9 us
    pallas_call x1, Pallas kernels, whole_grads(): pl.pallas_call(finish_kernel, out_shape=[jax.ShapeDtypeStruct((rows, cols...  1.2 us

profile of v5, /device:TPU:0, one launch (start us, length us, event | category | flops | bytes accessed | tf_op | source)
XLA Modules:
  0.0 39.8 jit_solution(15121420713272235846)
XLA Ops:
  0.6 37.9 %whole_grads.1 = (bf16[16,32,384]{2,1,0:T(8,128)(2,1)S(1)}, f32[768,384]{1,0:T(8,128)S(1)}, f32[12,225]{1,0:T(8,128)S(1)}, f32[12]{0:T(128)S(1)}, f32[384]{0:T(512)S(1)}) custom-call(bf16[1,16,32,384]{3,2,1,0:T(8,128)(2,1)} %tokens_ref.1, bf16[1,16,32,384]{3,2,1,0:T(8,128)(2,1)} %cot_ref.1, bf16[384,1152]{1,0:T(8,128)(2,1)} %w_qkv_hbm.1, ...), custom_call_target="tpu_custom_call" | custom-call | tf_op jit(solution)/shard_map/whole_grads/pallas_call | solution.py:976
  38.6 1.2 %finish.1 = (bf16[16,32,384]{2,1,0:T(8,128)(2,1)}, f32[576,384]{1,0:T(8,128)}, f32[192,384]{1,0:T(8,128)}, f32[12,225]{1,0:T(8,128)}, f32[12]{0:T(128)}, /*index=5*/f32[384]{0:T(512)}) custom-call(bf16[16,32,384]{2,1,0:T(8,128)(2,1)S(1)} %get-tuple-element.17.tok_ref, f32[768,384]{1,0:T(8,128)S(1)} %get-tuple-element.18.grads_ref, ...), custom_call_target="tpu_custom_call" | custom-call | tf_op jit(solution)/shard_map/finish/pallas_call | solution.py:1012

commit v6 on v5

--- a/solution.py
+++ b/solution.py
@@ -662,7 +662,7 @@
         flying[c].wait()
         core_mine[...] = core_mine[...] + core_get[...].astype(f32)
         w = plane_send.shape[1]
-        for k, (b, y, device) in enumerate(((1 - ba, wa, image), (ba, 1 - wa, side), (1 - ba, 1 - wa, corner))):
+        for k, (b, y, device) in enumerate(((1 - ba, 1 - wa, corner), (1 - ba, wa, image), (ba, 1 - wa, side))):
             place = pl.ds(pl.multiple_of((2 * b + y) * w, 32), w)
             plane_send[k] = core_mine[place, :].astype(b16)
             start(plane_send.at[k], plane_get.at[k], chunks[c][10], device)

time: 39.9 us -> 39.7 us (level)
  no operation moved by 1% of the time
where the time goes in v6:
time: 39.7 us; the launch traced here: 39.5 us
  Pallas kernels  38.9 us (98%)
  between operations  0.64 us (2%)
    pallas_call x1, Pallas kernels, whole_grads(): pl.pallas_call(functools.partial(whole_kernel, (size_h, size_w), height,...  37.7 us
    pallas_call x1, Pallas kernels, whole_grads(): pl.pallas_call(finish_kernel, out_shape=[jax.ShapeDtypeStruct((rows, cols...  1.2 us

profile of v6, /device:TPU:0, one launch (start us, length us, event | category | flops | bytes accessed | tf_op | source)
XLA Modules:
  0.0 39.5 jit_solution(13772778666290760398)
XLA Ops:
  0.6 37.7 %whole_grads.1 = (bf16[16,32,384]{2,1,0:T(8,128)(2,1)S(1)}, f32[768,384]{1,0:T(8,128)S(1)}, f32[12,225]{1,0:T(8,128)S(1)}, f32[12]{0:T(128)S(1)}, f32[384]{0:T(512)S(1)}) custom-call(bf16[1,16,32,384]{3,2,1,0:T(8,128)(2,1)} %tokens_ref.1, bf16[1,16,32,384]{3,2,1,0:T(8,128)(2,1)} %cot_ref.1, bf16[384,1152]{1,0:T(8,128)(2,1)} %w_qkv_hbm.1, ...), custom_call_target="tpu_custom_call" | custom-call | tf_op jit(solution)/shard_map/whole_grads/pallas_call | solution.py:976
  38.3 1.2 %finish.1 = (bf16[16,32,384]{2,1,0:T(8,128)(2,1)}, f32[576,384]{1,0:T(8,128)}, f32[192,384]{1,0:T(8,128)}, f32[12,225]{1,0:T(8,128)}, f32[12]{0:T(128)}, /*index=5*/f32[384]{0:T(512)}) custom-call(bf16[16,32,384]{2,1,0:T(8,128)(2,1)S(1)} %get-tuple-element.17.tok_ref, f32[768,384]{1,0:T(8,128)S(1)} %get-tuple-element.18.grads_ref, ...), custom_call_target="tpu_custom_call" | custom-call | tf_op jit(solution)/shard_map/finish/pallas_call | solution.py:1012
